TPU v7x, 32 devices: a whole 2x2x4 slice. The times are simulated.
32 devices in a mesh: dp: 8 (over z, core), ctx: 4 (over y, x).
Axes of the slice: x: 2, y: 2, z: 4, core: 2. Of those that a mesh axis runs over, the one named last changes fastest.
Arguments:
- state_rows: bfloat16 [12288, 2048], P(('dp', 'ctx')), parts along dimension 0, may hold values from -6 to 6
- query_vectors: bfloat16 [8, 12288, 128], P(None, ('dp', 'ctx')), parts along dimension 1, may hold values from -6 to 6
- key_vectors: bfloat16 [8, 12288, 128], P(None, ('dp', 'ctx')), parts along dimension 1, may hold values from -6 to 6
- value_vectors: bfloat16 [8, 12288, 128], P(None, ('dp', 'ctx')), parts along dimension 1, may hold values from -24 to 24
- halt_counts: int32 [12288], P(('dp', 'ctx')), parts along dimension 0, may hold values from 1 to 6, as said below
- out_weight: bfloat16 [8, 128, 2048], replicated, may hold values from -0.75 to 0.75
- norm_gain: bfloat16 [2048], replicated, may hold values from 0.099609375 to 1.8984375
Outputs:
- new_state: bfloat16 [12288, 2048], P(('dp', 'ctx')), parts along dimension 0
There are 8 independent parts, one for each index of `dp`. A program takes and returns all parts, laid end to end along the dimension named above; an argument that names none is the same for every part. Nothing has to cross between parts.
Inputs may be any that keep to these rules, and one draw needn't show every extreme that they name: halt_counts is equal within each aligned tile of 128 positions; exactly 3 tiles of a document have counts above 2, and on some device of ctx all 3 tiles do.
All inputs are finite; a program needn't handle non-finite values.
Results may differ from a plain program's by a relative error of at most 0.008.
Values may be sent and summed in bfloat16 or wider, within the bound.
A program may use at most 128 MiB of HBM per device.

v0:
```python
import functools

import jax
import jax.numpy as jnp
from jax import lax
from jax.experimental import pallas as pl
from jax.experimental.pallas import tpu as pltpu
from jax.sharding import PartitionSpec as P

STEP = 2
TILE = 128
LOG2E = 1.4426950408889634


def peer_of(me, step, n):
    peer = 0
    bit = 1
    while bit < n:
        digit = (me // bit) % 2
        if step & bit:
            digit = (digit + 1) % 2
        peer = peer + digit * bit
        bit *= 2
    return peer


def split_kernel(
    n,
    share,
    halt_ref,
    q_hbm,
    k_hbm,
    v_hbm,
    state_hbm,
    w_hbm,
    gain_ref,
    out_ref,
    q_buf,
    k_buf,
    v_buf,
    flag_out,
    flag_buf,
    state_buf,
    w_buf,
    probs,
    inv_sum,
    att_buf,
    update,
    send_sem,
    recv_sem,
    flag_send,
    flag_recv,
    att_send,
    att_recv,
    local_sem,
    w_sem,
    state_sem,
):
    me = lax.axis_index("ctx")
    rows, width = q_hbm.shape[1], q_hbm.shape[2]
    blocks = rows // TILE
    scale = width ** (-0.5) * LOG2E
    peers = [peer_of(me, step, n) for step in range(n)]
    order = list(range(n - 1, 0, -1))
    tensors = ((k_hbm, k_buf), (q_hbm, q_buf), (v_hbm, v_buf))
    own_rows = pl.ds(pl.multiple_of(me * rows, rows), rows)
    own_lanes = pl.ds(pl.multiple_of(me * width, width), width)

    flag = jnp.full(flag_out.shape, halt_ref[0] > STEP).astype(jnp.float32)
    flag_out[...] = flag

    own = {}
    for h in range(share):
        for index, (src, buf) in enumerate(tensors):
            own[index, h] = pltpu.make_async_copy(
                src.at[me * share + h], buf.at[h, own_rows], local_sem.at[index, h]
            )
            own[index, h].start()

    barrier = pltpu.get_barrier_semaphore()
    for step in range(1, n):
        pl.semaphore_signal(
            barrier, inc=1, device_id={"ctx": peers[step]}, device_id_type=pl.DeviceIdType.MESH
        )
    pl.semaphore_wait(barrier, n - 1)

    def remote(src, dst, send, recv, step):
        copy = pltpu.make_async_remote_copy(
            src_ref=src,
            dst_ref=dst,
            send_sem=send,
            recv_sem=recv,
            device_id={"ctx": peers[step]},
            device_id_type=pl.DeviceIdType.MESH,
        )
        copy.start()
        return copy

    sends, flags, gathers = {}, {}, {}
    for h in range(share):
        for index, (src, buf) in enumerate(tensors):
            for step in order:
                sends[index, h, step] = remote(
                    src.at[peers[step] * share + h],
                    buf.at[h, own_rows],
                    send_sem.at[index, h, step],
                    recv_sem.at[index, h, step],
                    step,
                )
            if h == 0 and index == 0:
                for step in order:
                    flags[step] = remote(
                        flag_out, flag_buf.at[me], flag_send.at[step], flag_recv.at[step], step
                    )

    w_copies = []
    for head in range(n * share):
        w_copies.append(
            pltpu.make_async_copy(
                w_hbm.at[head],
                w_buf.at[head % share, pl.ds((head // share) * width, width)],
                w_sem.at[head],
            )
        )
        w_copies[-1].start()
    state_copy = pltpu.make_async_copy(state_hbm, state_buf, state_sem)
    state_copy.start()

    def arrived(index, h):
        own[index, h].wait()
        for step in order:
            sends[index, h, step].wait_recv()

    def gather(h, block):
        if block is None:
            cut, slot = pl.ds(0, rows), 0
        else:
            cut, slot = pl.ds(block * TILE, TILE), block
        for step in order:
            gathers[h, slot, step] = remote(
                att_buf.at[h, cut, own_lanes],
                att_buf.at[h, cut, own_lanes],
                att_send.at[h, slot, step],
                att_recv.at[h, slot, step],
                step,
            )

    for h in range(share):
        arrived(0, h)
        arrived(1, h)
        if h == 0:
            for step in order:
                flags[step].wait_recv()
        for block in range(blocks):
            base = block * TILE
            chosen = q_buf[h, pl.ds(pl.multiple_of(me * rows, rows) + base, TILE), :].astype(jnp.float32) * flag[0:1, :]
            for step in order:
                start = pl.multiple_of(peers[step] * rows, rows) + base
                term = q_buf[h, pl.ds(start, TILE), :].astype(jnp.float32)
                chosen = chosen + term * flag_buf[peers[step], 0:1, :]
            scores = lax.dot_general(
                chosen.astype(jnp.bfloat16),
                k_buf[h],
                (((1,), (1,)), ((), ())),
                preferred_element_type=jnp.float32,
            )
            top = jnp.max(scores, axis=1, keepdims=True)
            weights = jnp.exp2((scores - top) * scale)
            total = jnp.sum(weights, axis=1, keepdims=True)
            probs[base : base + TILE, :] = weights.astype(jnp.bfloat16)
            inv_sum[base : base + TILE, :] = jnp.broadcast_to(1.0 / total, (TILE, width))
        arrived(2, h)
        last = h == share - 1
        for block in range(blocks):
            cut = slice(block * TILE, (block + 1) * TILE)
            weighted = jnp.dot(probs[cut, :], v_buf[h], preferred_element_type=jnp.float32)
            att_buf[h, cut, own_lanes] = (weighted * inv_sum[cut, :]).astype(jnp.bfloat16)
            if last:
                gather(h, block)
        if not last:
            gather(h, None)

    for copy in w_copies:
        copy.wait()
    state_copy.wait()

    for h in range(share - 1):
        for step in order:
            gathers[h, 0, step].wait_recv()

        def body(block, carry, h=h):
            cut = pl.ds(pl.multiple_of(block * TILE, TILE), TILE)
            product = jnp.dot(att_buf[h, cut, :], w_buf[h], preferred_element_type=jnp.float32)
            if h == 0:
                update[cut, :] = state_buf[cut, :].astype(jnp.float32) + product
            else:
                update[cut, :] = update[cut, :] + product
            return carry

        lax.fori_loop(0, blocks, body, 0)

    gain = gain_ref[...].astype(jnp.float32).reshape(1, -1)
    h = share - 1
    for block in range(blocks):
        for step in order:
            gathers[h, block, step].wait_recv()
        cut = slice(block * TILE, (block + 1) * TILE)
        mixed = jnp.dot(att_buf[h, cut, :], w_buf[h], preferred_element_type=jnp.float32)
        residual = update if share > 1 else state_buf
        mixed = residual[cut, :].astype(jnp.float32) + mixed
        mean = jnp.mean(mixed * mixed, axis=-1, keepdims=True)
        normed = mixed * lax.rsqrt(mean + 1e-06) * gain
        active = jnp.full(normed.shape, halt_ref[block * TILE] > STEP)
        kept = state_buf[cut, :].astype(jnp.float32)
        out_ref[cut, :] = jnp.where(active, normed, kept).astype(out_ref.dtype)

    for group in (sends, flags, gathers):
        for copy in group.values():
            copy.wait_send()


def split_heads(n, state_rows, q, k, v, halt_counts, out_weight, norm_gain):
    heads, rows, width = q.shape
    share = heads // n
    features = state_rows.shape[1]
    bf16, f32 = jnp.bfloat16, jnp.float32
    hbm = pl.BlockSpec(memory_space=pltpu.MemorySpace.HBM)
    vmem = pl.BlockSpec(memory_space=pltpu.VMEM)
    block = pltpu.VMEM((share, n * rows, width), bf16)
    dma = pltpu.SemaphoreType.DMA
    new_state = pl.pallas_call(
        functools.partial(split_kernel, n, share),
        out_shape=jax.ShapeDtypeStruct((rows, features), bf16),
        in_specs=[pl.BlockSpec(memory_space=pltpu.SMEM)] + [hbm] * 5 + [vmem],
        out_specs=vmem,
        scratch_shapes=[
            block,
            block,
            block,
            pltpu.VMEM((8, 128), f32),
            pltpu.VMEM((n, 8, 128), f32),
            pltpu.VMEM((rows, features), bf16),
            pltpu.VMEM((share, n * width, features), bf16),
            pltpu.VMEM((rows, n * rows), bf16),
            pltpu.VMEM((rows, width), f32),
            pltpu.VMEM((share, rows, n * width), bf16),
            pltpu.VMEM((rows, features), f32),
            dma((3, share, n)),
            dma((3, share, n)),
            dma((n,)),
            dma((n,)),
            dma((share, rows // TILE, n)),
            dma((share, rows // TILE, n)),
            dma((3, share)),
            dma((heads,)),
            dma,
        ],
        compiler_params=pltpu.CompilerParams(
            collective_id=0, has_side_effects=True, vmem_limit_bytes=60 * 1024 * 1024
        ),
    )(halt_counts, q, k, v, state_rows, out_weight, norm_gain)
    return new_state


def fold_heads(carry, queries, key_piece, value_piece, score_scale):
    running_max, running_sum, weighted = carry

    def per_head(head_items):
        query_head, key_head, value_head, max_head, sum_head, weighted_head = head_items
        scores = (
            lax.dot_general(
                query_head, key_head, (((1,), (1,)), ((), ())), preferred_element_type=jnp.float32
            )
            * score_scale
        )
        new_max = jnp.maximum(max_head, jnp.max(scores, axis=1))
        shrink = jnp.exp(max_head - new_max)
        exponents = jnp.exp(scores - new_max[:, None])
        sum_head = sum_head * shrink + jnp.sum(exponents, axis=1)
        weighted_head = weighted_head * shrink[:, None] + jnp.dot(
            exponents.astype(jnp.bfloat16), value_head, preferred_element_type=jnp.float32
        )
        return (new_max, sum_head, weighted_head)

    return lax.map(per_head, (queries, key_piece, value_piece, running_max, running_sum, weighted))


def empty_carry(head_count, query_count, head_width):
    return (
        jnp.full((head_count, query_count), -1e30, jnp.float32),
        jnp.zeros((head_count, query_count), jnp.float32),
        jnp.zeros((head_count, query_count, head_width), jnp.float32),
    )


def attend_keys(query_vectors, key_vectors, value_vectors, score_scale):
    head_count, row_count, head_width = query_vectors.shape
    initial = empty_carry(head_count, row_count, head_width)
    running_max, running_sum, weighted = fold_heads(
        initial,
        query_vectors,
        lax.all_gather(key_vectors, "ctx", axis=1, tiled=True),
        lax.all_gather(value_vectors, "ctx", axis=1, tiled=True),
        score_scale,
    )
    return (weighted / running_sum[..., None]).astype(jnp.bfloat16)


def on_device(
    state_rows, query_vectors, key_vectors, value_vectors, halt_counts, out_weight, norm_gain
):
    head_count, row_count, head_width = query_vectors.shape
    score_scale = head_width ** (-0.5)
    attended = attend_keys(query_vectors, key_vectors, value_vectors, score_scale)
    update = jnp.einsum("hqd,hde->qe", attended, out_weight, preferred_element_type=jnp.float32)
    mixed_sum = state_rows.astype(jnp.float32) + update
    normed = (
        mixed_sum
        * lax.rsqrt(jnp.mean(mixed_sum * mixed_sum, axis=-1, keepdims=True) + 1e-06)
        * norm_gain.astype(jnp.float32)
    )
    active = (halt_counts > STEP)[:, None]
    return jnp.where(active, normed.astype(jnp.bfloat16), state_rows)


def solution(mesh):
    n_ctx = mesh.shape["ctx"]

    def per_device(state_rows, q, k, v, halt_counts, out_weight, norm_gain):
        heads, rows, _ = q.shape
        one_owner = rows == (n_ctx - 1) * TILE
        if one_owner and heads % n_ctx == 0 and n_ctx & (n_ctx - 1) == 0:
            return split_heads(n_ctx, state_rows, q, k, v, halt_counts, out_weight, norm_gain)
        return on_device(state_rows, q, k, v, halt_counts, out_weight, norm_gain)

    placed = (
        P(("dp", "ctx"), None),
        P(None, ("dp", "ctx"), None),
        P(None, ("dp", "ctx"), None),
        P(None, ("dp", "ctx"), None),
        P(("dp", "ctx")),
        P(),
        P(),
    )
    return jax.shard_map(
        per_device, mesh=mesh, in_specs=placed, out_specs=P(("dp", "ctx"), None), check_vma=False
    )
```

profile of v0, /device:TPU:0, one launch (start us, length us, event | category | flops | bytes accessed | tf_op | source)
XLA Modules:
  0.0 45.4 jit_solution(11139045484995256700)
XLA Ops:
  0.0 42.7 %shard_map.73 = bf16[384,2048]{1,0:T(8,128)(2,1)} custom-call(s32[384]{0:T(512)} %halt_ref.1, bf16[8,384,128]{2,1,0:T(8,128)(2,1)} %q_hbm.1, bf16[8,384,128]{2,1,0:T(8,128)(2,1)} %k_hbm.1, bf16[8,384,128]{2,1,0:T(8,128)(2,1)} %v_hbm.1, bf16[384,2048]{1,0:T(8,128)(2,1)} %state_hbm.1, bf16[8,128,2048]{2,1,0:T(8,128)(2,1)} %w_hbm.1, bf16[2048]{0:T(1024)(128)(2,1)} %gain_ref.1), custom_call_target="tpu_custom_call" | custom-call | tf_op jit(solution)/shard_map/pallas_call | solution.py:231
  42.7 2.7 %copy.9 = bf16[384,2048]{1,0:T(8,128)(2,1)} copy(bf16[384,2048]{1,0:T(8,128)(2,1)} %shard_map.73) | data formatting | bytes 3145728
where the time goes:
time: 45.6 us; the launch traced here: 45.4 us
  Pallas kernels  42.7 us (94%)
  local copies, waits for them, and re-layouts  2.73 us (6%)
    pallas_call x1, Pallas kernels, split_heads(): pl.pallas_call(functools.partial(split_kernel, n, share), out_shape=jax.S...  42.7 us
    unnamed x1, local copies, waits for them, and re-layouts  2.73 us

commit v1 on v0

--- a/solution.py
+++ b/solution.py
@@ -256,9 +256,9 @@
             dma,
         ],
         compiler_params=pltpu.CompilerParams(
-            collective_id=0, has_side_effects=True, vmem_limit_bytes=60 * 1024 * 1024
+            collective_id=0, has_side_effects=True, vmem_limit_bytes=24 * 1024 * 1024
         ),
-    )(halt_counts, q, k, v, state_rows, out_weight, norm_gain)
+    )(halt_counts, *[pltpu.with_memory_space_constraint(x, pltpu.HBM) for x in (q, k, v, state_rows, out_weight)], norm_gain)
     return new_state
 
 

time: 45.6 us -> 44.1 us (0.967)
  Pallas kernels: 42.7 us -> 41.4 us
    pallas_call x1, Pallas kernels: 42.7 us -> 41.4 us  [split_heads(): pl.pallas_call(functools.partial(split_kernel, n, share), out_shape=jax.S...]
    unnamed x1 -> x5, local copies, waits for them, and re-layouts: 2.73 us -> 2.51 us
where the time goes in v1:
time: 44.1 us; the launch traced here: 43.9 us
  Pallas kernels  41.4 us (94%)
  local copies, waits for them, and re-layouts  2.51 us (6%)
    pallas_call x1, Pallas kernels, split_heads(): pl.pallas_call(functools.partial(split_kernel, n, share), out_shape=jax.S...  41.4 us
    unnamed x5, local copies, waits for them, and re-layouts  2.51 us

profile of v1, /device:TPU:0, one launch (start us, length us, event | category | flops | bytes accessed | tf_op | source)
XLA Modules:
  0.0 43.9 jit_solution(17628897820151769793)
XLA Ops:
  0.0 0.0 copy-start
  0.0 0.7 %copy-done = bf16[2048]{0:T(1024)(128)(2,1)S(1)} copy-done((bf16[2048]{0:T(1024)(128)(2,1)S(1)}, bf16[2048]{0:T(1024)(128)(2,1)}, u32[]{:S(2)}) %copy-start) | copy-done | bytes 4120
  0.7 0.0 copy-start.1
  0.7 0.7 %copy-done.1 = s32[384]{0:T(512)S(1)} copy-done((s32[384]{0:T(512)S(1)}, s32[384]{0:T(512)}, u32[]{:S(2)}) %copy-start.1) | copy-done | bytes 1560
  1.4 41.4 %shard_map.73 = bf16[384,2048]{1,0:T(8,128)(2,1)S(1)} custom-call(s32[384]{0:T(512)S(1)} %copy-done.1, bf16[8,384,128]{2,1,0:T(8,128)(2,1)} %q_hbm.1, bf16[8,384,128]{2,1,0:T(8,128)(2,1)} %k_hbm.1, bf16[8,384,128]{2,1,0:T(8,128)(2,1)} %v_hbm.1, bf16[384,2048]{1,0:T(8,128)(2,1)} %state_hbm.1, bf16[8,128,2048]{2,1,0:T(8,128)(2,1)} %w_hbm.1, ...), custom_call_target="tpu_custom_call" | custom-call | tf_op jit(solution)/shard_map/pallas_call | solution.py:231
  42.8 1.1 %copy.9 = bf16[384,2048]{1,0:T(8,128)(2,1)} copy(bf16[384,2048]{1,0:T(8,128)(2,1)S(1)} %shard_map.73) | data formatting | bytes 3145728
Async XLA Ops:
  0.0 0.7 %copy-start = (bf16[2048]{0:T(1024)(128)(2,1)S(1)}, bf16[2048]{0:T(1024)(128)(2,1)}, u32[]{:S(2)}) copy-start(bf16[2048]{0:T(1024)(128)(2,1)} %gain_ref.1) | copy-start | bytes 12292
  0.7 0.7 %copy-start.1 = (s32[384]{0:T(512)S(1)}, s32[384]{0:T(512)}, u32[]{:S(2)}) copy-start(s32[384]{0:T(512)} %halt_ref.1) | copy-start | bytes 4612

commit v2 on v1

v2 whole, which is shorter than its diff:
```python
import functools

import jax
import jax.numpy as jnp
from jax import lax
from jax.experimental import pallas as pl
from jax.experimental.pallas import tpu as pltpu
from jax.sharding import PartitionSpec as P

STEP = 2
TILE = 128
LOG2E = 1.4426950408889634


def square_kernel(
    share,
    halt_hbm,
    q_hbm,
    k_hbm,
    v_hbm,
    state_hbm,
    w_hbm,
    gain_hbm,
    out_ref,
    halt,
    gain_buf,
    q_buf,
    q_near,
    q_mid,
    q_far,
    k_buf,
    v_buf,
    own_acc,
    own_stat,
    part_out,
    part_in,
    stat_out,
    stat_in,
    att_own,
    att_in,
    state_buf,
    w_own,
    w_in,
    update,
    halt_sem,
    gain_sem,
    state_sem,
    q_sem,
    kv_sem,
    w_sem,
    send_sem,
    recv_sem,
):
    me = lax.axis_index("ctx")
    bits = (me % 2, me // 2)
    peer = (bits[1] * 2 + 1 - bits[0], (1 - bits[1]) * 2 + bits[0])
    rows, width = q_hbm.shape[1], q_hbm.shape[2]
    features = state_hbm.shape[1]
    scale = width ** (-0.5) * LOG2E
    axes = (0, 1)

    def head(s, a, owner):
        side = bits[s] if owner == 0 else 1 - bits[s]
        return (s * 2 + side) * share + a

    def local(src, dst, sem):
        copy = pltpu.make_async_copy(src, dst, sem)
        copy.start()
        return copy

    def remote(src, dst, kind, s, a, axis):
        copy = pltpu.make_async_remote_copy(
            src_ref=src,
            dst_ref=dst,
            send_sem=send_sem.at[kind, s, a],
            recv_sem=recv_sem.at[kind, s, a],
            device_id={"ctx": peer[axis]},
            device_id_type=pl.DeviceIdType.MESH,
        )
        copy.start()
        copies.append(copy)
        return copy

    copies = []
    halt_copy = local(halt_hbm, halt, halt_sem)
    q_copy = {}
    for owner in (1, 0):
        for a in range(share):
            for s in axes:
                q_copy[s, a, owner] = local(
                    q_hbm.at[head(s, a, owner)], q_buf.at[s, a, owner], q_sem.at[s, a, owner]
                )

    barrier = pltpu.get_barrier_semaphore()
    for s in axes:
        pl.semaphore_signal(
            barrier, inc=1, device_id={"ctx": peer[s]}, device_id_type=pl.DeviceIdType.MESH
        )

    halt_copy.wait()
    flag = jnp.full((1, width), halt[0] > STEP).astype(jnp.bfloat16)

    near, far, keys, values, parts, stats, gathers = {}, {}, {}, {}, {}, {}, {}
    for a in range(share):
        for s in axes:
            q_copy[s, a, 1].wait()
            q_buf[s, a, 1] = q_buf[s, a, 1] * flag
    pl.semaphore_wait(barrier, 2)

    def send_keys(a):
        for s in axes:
            keys[s, a] = remote(k_hbm.at[head(s, a, 1)], k_buf.at[s, a, 1], 2, s, a, s)

    def send_values(a):
        for s in axes:
            values[s, a] = remote(v_hbm.at[head(s, a, 1)], v_buf.at[s, a, 1], 3, s, a, s)

    def pass_on(a):
        for s in axes:
            q_copy[s, a, 0].wait()
            near[s, a].wait_recv()
            q_mid[s, a] = q_buf[s, a, 0] * flag + q_near[s, a]
            far[s, a] = remote(q_mid.at[s, a], q_far.at[s, a], 1, s, a, 1 - s)

    for a in range(share):
        for s in axes:
            near[s, a] = remote(q_buf.at[s, a, 1], q_near.at[s, a], 0, s, a, s)
    send_keys(0)

    own_kv = {}
    for a in range(share):
        for s in axes:
            for i, (src, buf) in enumerate(((k_hbm, k_buf), (v_hbm, v_buf))):
                own_kv[i, s, a] = local(
                    src.at[head(s, a, 0)], buf.at[s, a, 0], kv_sem.at[i, s, a]
                )
    w_copies = []
    for a in range(share):
        for owner, buf in enumerate((w_own, w_in)):
            for s in axes:
                w_copies.append(
                    local(
                        w_hbm.at[head(s, a, owner)],
                        buf.at[a, pl.ds(s * width, width)],
                        w_sem.at[owner, s, a],
                    )
                )
    state_copy = local(state_hbm, state_buf, state_sem)
    gain_copy = local(gain_hbm, gain_buf, gain_sem)

    for a in range(share):
        pass_on(a)
        send_values(a)
        if a + 1 < share:
            send_keys(a + 1)

    def attend(s, a):
        far[s, a].wait_recv()
        own_kv[0, s, a].wait()
        keys[s, a].wait_recv()
        query = q_mid[s, a] + q_far[s, a]
        scores = lax.dot_general(
            k_buf[s, a].reshape(2 * rows, width),
            query,
            (((1,), (1,)), ((), ())),
            preferred_element_type=jnp.float32,
        )
        top = jnp.max(scores, axis=0, keepdims=True)
        weights = jnp.exp2((scores - top) * scale)
        total = jnp.sum(weights, axis=0, keepdims=True)
        own_kv[1, s, a].wait()
        values[s, a].wait_recv()
        weighted = lax.dot_general(
            v_buf[s, a].reshape(2 * rows, width),
            weights.astype(jnp.bfloat16),
            (((0,), (0,)), ((), ())),
            preferred_element_type=jnp.float32,
        )
        stat = jnp.concatenate([top, total], axis=0)
        own_acc[s, a] = weighted
        own_stat[s, a] = stat
        part_out[s, a] = (weighted * (1.0 / total)).astype(jnp.bfloat16)
        stat_out[s, a] = stat
        parts[s, a] = remote(part_out.at[s, a], part_in.at[s, a], 4, s, a, 1 - s)
        stats[s, a] = remote(stat_out.at[s, a], stat_in.at[s, a], 5, s, a, 1 - s)

    def combine(s, a):
        parts[s, a].wait_recv()
        stats[s, a].wait_recv()
        top, total = own_stat[s, a, 0:1], own_stat[s, a, 1:2]
        top_in, total_in = stat_in[s, a, 0:1], stat_in[s, a, 1:2]
        both = jnp.maximum(top, top_in)
        shrink = jnp.exp2((top - both) * scale)
        total_in = total_in * jnp.exp2((top_in - both) * scale)
        inverse = 1.0 / (total * shrink + total_in)
        attended = own_acc[s, a] * (shrink * inverse)
        attended = attended + part_in[s, a].astype(jnp.float32) * (total_in * inverse)
        att_own[s, a] = attended.T.astype(jnp.bfloat16)
        gathers[s, a] = remote(att_own.at[s, a], att_in.at[s, a], 6, s, a, s)

    def both_axes(buf, a, cut):
        return jnp.concatenate([buf[s, a, cut] for s in axes], axis=1)

    chunk = min(4 * TILE, features)

    def project(buf, weight, a, first):
        left = both_axes(buf, a, slice(None))

        def body(step, carry):
            cut = pl.ds(pl.multiple_of(step * chunk, chunk), chunk)
            product = jnp.dot(left, weight[a, :, cut], preferred_element_type=jnp.float32)
            if first:
                update[:, cut] = state_buf[:, cut].astype(jnp.float32) + product
            else:
                update[:, cut] = update[:, cut] + product
            return carry

        lax.fori_loop(0, features // chunk, body, 0)

    for a in range(share):
        for s in axes:
            attend(s, a)
    for copy in w_copies:
        copy.wait()
    state_copy.wait()
    gain_copy.wait()
    for a in range(share):
        for s in axes:
            combine(s, a)
        project(att_own, w_own, a, a == 0)
    for a in range(share - 1):
        for s in axes:
            gathers[s, a].wait_recv()
        project(att_in, w_in, a, False)

    gain = gain_buf[...].astype(jnp.float32).reshape(1, -1)
    a = share - 1
    for s in axes:
        gathers[s, a].wait_recv()
    for block in range(rows // TILE):
        cut = slice(block * TILE, (block + 1) * TILE)
        product = jnp.dot(both_axes(att_in, a, cut), w_in[a], preferred_element_type=jnp.float32)
        mixed = update[cut, :] + product
        mean = jnp.mean(mixed * mixed, axis=-1, keepdims=True)
        normed = mixed * lax.rsqrt(mean + 1e-06) * gain
        active = jnp.full(normed.shape, halt[block * TILE] > STEP)
        kept = state_buf[cut, :].astype(jnp.float32)
        out_ref[cut, :] = jnp.where(active, normed, kept).astype(out_ref.dtype)

    for copy in copies:
        copy.wait_send()


def on_square(state_rows, q, k, v, halt_counts, out_weight, norm_gain):
    heads, rows, width = q.shape
    share = heads // 4
    features = state_rows.shape[1]
    bf16, f32 = jnp.bfloat16, jnp.float32
    hbm = pl.BlockSpec(memory_space=pltpu.MemorySpace.HBM)
    vmem = pl.BlockSpec(memory_space=pltpu.VMEM)
    dma = pltpu.SemaphoreType.DMA
    operands = (halt_counts, q, k, v, state_rows, out_weight, norm_gain)
    return pl.pallas_call(
        functools.partial(square_kernel, share),
        out_shape=jax.ShapeDtypeStruct((rows, features), bf16),
        in_specs=[hbm] * len(operands),
        out_specs=vmem,
        scratch_shapes=[
            pltpu.SMEM((rows,), jnp.int32),
            pltpu.VMEM((features,), bf16),
            pltpu.VMEM((2, share, 2, rows, width), bf16),
            pltpu.VMEM((2, share, rows, width), bf16),
            pltpu.VMEM((2, share, rows, width), bf16),
            pltpu.VMEM((2, share, rows, width), bf16),
            pltpu.VMEM((2, share, 2, rows, width), bf16),
            pltpu.VMEM((2, share, 2, rows, width), bf16),
            pltpu.VMEM((2, share, width, rows), f32),
            pltpu.VMEM((2, share, 2, rows), f32),
            pltpu.VMEM((2, share, width, rows), bf16),
            pltpu.VMEM((2, share, width, rows), bf16),
            pltpu.VMEM((2, share, 2, rows), f32),
            pltpu.VMEM((2, share, 2, rows), f32),
            pltpu.VMEM((2, share, rows, width), bf16),
            pltpu.VMEM((2, share, rows, width), bf16),
            pltpu.VMEM((rows, features), bf16),
            pltpu.VMEM((share, 2 * width, features), bf16),
            pltpu.VMEM((share, 2 * width, features), bf16),
            pltpu.VMEM((rows, features), f32),
            dma,
            dma,
            dma,
            dma((2, share, 2)),
            dma((2, 2, share)),
            dma((2, 2, share)),
            dma((7, 2, share)),
            dma((7, 2, share)),
        ],
        compiler_params=pltpu.CompilerParams(
            collective_id=0, has_side_effects=True, vmem_limit_bytes=28 * 1024 * 1024
        ),
    )(*[pltpu.with_memory_space_constraint(x, pltpu.HBM) for x in operands])


def fold_heads(carry, queries, key_piece, value_piece, score_scale):
    running_max, running_sum, weighted = carry

    def per_head(head_items):
        query_head, key_head, value_head, max_head, sum_head, weighted_head = head_items
        scores = (
            lax.dot_general(
                query_head, key_head, (((1,), (1,)), ((), ())), preferred_element_type=jnp.float32
            )
            * score_scale
        )
        new_max = jnp.maximum(max_head, jnp.max(scores, axis=1))
        shrink = jnp.exp(max_head - new_max)
        exponents = jnp.exp(scores - new_max[:, None])
        sum_head = sum_head * shrink + jnp.sum(exponents, axis=1)
        weighted_head = weighted_head * shrink[:, None] + jnp.dot(
            exponents.astype(jnp.bfloat16), value_head, preferred_element_type=jnp.float32
        )
        return (new_max, sum_head, weighted_head)

    return lax.map(per_head, (queries, key_piece, value_piece, running_max, running_sum, weighted))


def empty_carry(head_count, query_count, head_width):
    return (
        jnp.full((head_count, query_count), -1e30, jnp.float32),
        jnp.zeros((head_count, query_count), jnp.float32),
        jnp.zeros((head_count, query_count, head_width), jnp.float32),
    )


def attend_keys(query_vectors, key_vectors, value_vectors, score_scale):
    head_count, row_count, head_width = query_vectors.shape
    initial = empty_carry(head_count, row_count, head_width)
    running_max, running_sum, weighted = fold_heads(
        initial,
        query_vectors,
        lax.all_gather(key_vectors, "ctx", axis=1, tiled=True),
        lax.all_gather(value_vectors, "ctx", axis=1, tiled=True),
        score_scale,
    )
    return (weighted / running_sum[..., None]).astype(jnp.bfloat16)


def on_device(
    state_rows, query_vectors, key_vectors, value_vectors, halt_counts, out_weight, norm_gain
):
    head_count, row_count, head_width = query_vectors.shape
    score_scale = head_width ** (-0.5)
    attended = attend_keys(query_vectors, key_vectors, value_vectors, score_scale)
    update = jnp.einsum("hqd,hde->qe", attended, out_weight, preferred_element_type=jnp.float32)
    mixed_sum = state_rows.astype(jnp.float32) + update
    normed = (
        mixed_sum
        * lax.rsqrt(jnp.mean(mixed_sum * mixed_sum, axis=-1, keepdims=True) + 1e-06)
        * norm_gain.astype(jnp.float32)
    )
    active = (halt_counts > STEP)[:, None]
    return jnp.where(active, normed.astype(jnp.bfloat16), state_rows)


def solution(mesh):
    n_ctx = mesh.shape["ctx"]

    def per_device(state_rows, q, k, v, halt_counts, out_weight, norm_gain):
        heads, rows, _ = q.shape
        one_owner = rows == (n_ctx - 1) * TILE
        if one_owner and heads % n_ctx == 0 and n_ctx == 4:
            return on_square(state_rows, q, k, v, halt_counts, out_weight, norm_gain)
        return on_device(state_rows, q, k, v, halt_counts, out_weight, norm_gain)

    placed = (
        P(("dp", "ctx"), None),
        P(None, ("dp", "ctx"), None),
        P(None, ("dp", "ctx"), None),
        P(None, ("dp", "ctx"), None),
        P(("dp", "ctx")),
        P(),
        P(),
    )
    return jax.shard_map(
        per_device, mesh=mesh, in_specs=placed, out_specs=P(("dp", "ctx"), None), check_vma=False
    )
```

time: 44.1 us -> 35.4 us (0.80)
  Pallas kernels: 41.4 us -> 34.1 us
  local copies, waits for them, and re-layouts: 2.51 us -> 1.15 us
    pallas_call x1, Pallas kernels: 41.4 us -> 34.1 us  [on_square(): pl.pallas_call(functools.partial(square_kernel, share), out_shape=jax.Sha...]
    unnamed x5 -> x1, local copies, waits for them, and re-layouts: 2.51 us -> 1.15 us
where the time goes in v2:
time: 35.4 us; the launch traced here: 35.3 us
  Pallas kernels  34.1 us (96%)
  local copies, waits for them, and re-layouts  1.15 us (3%)
    pallas_call x1, Pallas kernels, on_square(): pl.pallas_call(functools.partial(square_kernel, share), out_shape=jax.Sha...  34.1 us
    unnamed x1, local copies, waits for them, and re-layouts  1.15 us

profile of v2, /device:TPU:0, one launch (start us, length us, event | category | flops | bytes accessed | tf_op | source)
XLA Modules:
  0.0 35.3 jit_solution(3899474332605060061)
XLA Ops:
  0.0 34.1 %shard_map.73 = bf16[384,2048]{1,0:T(8,128)(2,1)S(1)} custom-call(s32[384]{0:T(512)} %halt_hbm.1, bf16[8,384,128]{2,1,0:T(8,128)(2,1)} %q_hbm.1, bf16[8,384,128]{2,1,0:T(8,128)(2,1)} %k_hbm.1, bf16[8,384,128]{2,1,0:T(8,128)(2,1)} %v_hbm.1, bf16[384,2048]{1,0:T(8,128)(2,1)} %state_hbm.1, bf16[8,128,2048]{2,1,0:T(8,128)(2,1)} %w_hbm.1, bf16[2048]{0:T(1024)(128)(2,1)} %gain_hbm.1), custom_call_target="tpu_custom_call" | custom-call | tf_op jit(solution)/shard_map/pallas_call | solution.py:263
  34.1 1.1 %copy.9 = bf16[384,2048]{1,0:T(8,128)(2,1)} copy(bf16[384,2048]{1,0:T(8,128)(2,1)S(1)} %shard_map.73) | data formatting | bytes 3145728

commit v3 on v2

v3 whole, which is shorter than its diff:
```python
import functools

import jax
import jax.numpy as jnp
from jax import lax
from jax.experimental import pallas as pl
from jax.experimental.pallas import tpu as pltpu
from jax.sharding import PartitionSpec as P

STEP = 2
TILE = 128
LAG = 3
LOG2E = 1.4426950408889634


def star_kernel(
    halt_hbm,
    q_hbm,
    k_hbm,
    v_hbm,
    state_hbm,
    w_hbm,
    gain_hbm,
    out_ref,
    halt,
    gain_buf,
    flag_out,
    flag_in,
    q_buf,
    k_buf,
    v_buf,
    slot_out,
    slot_in,
    stat_out,
    stat_in,
    own_acc,
    att_buf,
    state_buf,
    w_buf,
    update,
    halt_sem,
    gain_sem,
    state_sem,
    qkv_sem,
    w_sem,
    flag_send,
    flag_recv,
    slot_send,
    slot_recv,
    stat_send,
    stat_recv,
):
    me = lax.axis_index("ctx")
    bits = (me % 2, me // 2)
    peer = (bits[1] * 2 + 1 - bits[0], (1 - bits[1]) * 2 + bits[0])
    heads, rows, width = q_hbm.shape
    features = state_hbm.shape[1]
    half = heads // 2
    blocks = rows // TILE
    scale = width ** (-0.5) * LOG2E
    axes = (0, 1)
    f32, bf16 = jnp.float32, jnp.bfloat16

    def local(src, dst, sem):
        copy = pltpu.make_async_copy(src, dst, sem)
        copy.start()
        return copy

    copies = []

    def remote(src, dst, send, recv, axis):
        copy = pltpu.make_async_remote_copy(
            src_ref=src,
            dst_ref=dst,
            send_sem=send,
            recv_sem=recv,
            device_id={"ctx": peer[axis]},
            device_id_type=pl.DeviceIdType.MESH,
        )
        copy.start()
        copies.append(copy)
        return copy

    def near_head(s, axis):
        return s // 2 + (half if (s + axis) % 2 == 0 else 0)

    halt_copy = local(halt_hbm, halt, halt_sem)
    own = {}
    for i in range(half):
        for h in (half + i, i):
            for n, (src, buf) in enumerate(((q_hbm, q_buf), (k_hbm, k_buf), (v_hbm, v_buf))):
                own[n, h] = local(src.at[h], buf.at[h], qkv_sem.at[n, h])
    loaded = set()

    def ready(n, h):
        if (n, h) not in loaded:
            own[n, h].wait()
            loaded.add((n, h))

    barrier = pltpu.get_barrier_semaphore()
    for axis in axes:
        pl.semaphore_signal(
            barrier, inc=1, device_id={"ctx": peer[axis]}, device_id_type=pl.DeviceIdType.MESH
        )
    halt_copy.wait()
    flag = jnp.full(flag_out.shape, halt[0] > STEP).astype(f32)
    flag_out[...] = flag

    def mask(value):
        return jnp.broadcast_to(value[0:1, :].astype(bf16), (rows, width)) > 0.5

    is_owner = mask(flag)

    def early(s, axis):
        h = near_head(s, axis)
        other = s // 2 + (half if axis == 0 else 0)
        ready(0, h)
        ready(1 + s % 2, other)
        return jnp.where(is_owner, q_buf[h], (k_buf, v_buf)[s % 2][other])

    slots, stats = {}, {}

    def send(s, axis):
        slots[s, axis] = remote(
            slot_out.at[s, axis],
            slot_in.at[s, axis],
            slot_send.at[s, axis],
            slot_recv.at[s, axis],
            axis,
        )

    for s in range(LAG):
        for axis in axes:
            slot_out[s, axis] = early(s, axis).reshape(blocks, TILE, width)
        if s == 0:
            pl.semaphore_wait(barrier, 2)
            flags = [
                remote(flag_out, flag_in.at[axis], flag_send.at[axis], flag_recv.at[axis], axis)
                for axis in axes
            ]
        for axis in axes:
            send(s, axis)

    w_copies = []
    for i in range(half):
        for side in (0, 1):
            w_copies.append(
                local(
                    w_hbm.at[i + side * half],
                    w_buf.at[i, pl.ds(side * width, width)],
                    w_sem.at[i, side],
                )
            )
    state_copy = local(state_hbm, state_buf, state_sem)
    gain_copy = local(gain_hbm, gain_buf, gain_sem)

    for axis in axes:
        flags[axis].wait_recv()
    owner_at = [mask(flag_in[axis]) for axis in axes]
    beside = flag_in[0] + flag_in[1]
    is_beside = mask(beside)
    bias = jnp.concatenate([(beside[0:1, :] - 1.0) * 1e30] * blocks, axis=1)

    def received(s, axis):
        return slot_in[s, axis].reshape(rows, width)

    def step(s):
        i = s // 2
        low, high = (i, half + i) if s % 2 == 0 else (half + i, i)
        for n in range(3):
            ready(n, low)
            ready(n, high)
        query = jnp.where(
            owner_at[0], received(s, 0), jnp.where(owner_at[1], received(s, 1), q_buf[low])
        )
        key = jnp.where(owner_at[0], k_buf[high], k_buf[low])
        value = jnp.where(owner_at[0], v_buf[high], v_buf[low])

        def score(keys):
            return lax.dot_general(
                keys, query, (((1,), (1,)), ((), ())), preferred_element_type=f32
            )

        def weigh(values, weights):
            return lax.dot_general(
                values, weights.astype(bf16), (((0,), (0,)), ((), ())), preferred_element_type=f32
            )

        scores = score(key)
        top = jnp.max(scores, axis=0, keepdims=True)
        if s % 2 == 1:
            far_key = jnp.where(owner_at[0], received(s - 1, 1), received(s - 1, 0))
            far_value = jnp.where(owner_at[0], received(s, 1), received(s, 0))
            far_value = jnp.where(is_beside, far_value, jnp.zeros_like(far_value))
            far_scores = score(far_key) + bias
            top = jnp.maximum(top, jnp.max(far_scores, axis=0, keepdims=True))
        weights = jnp.exp2((scores - top) * scale)
        total = jnp.sum(weights, axis=0, keepdims=True)
        weighted = weigh(value, weights)
        if s % 2 == 1:
            far_weights = jnp.exp2((far_scores - top) * scale)
            total = total + jnp.sum(far_weights, axis=0, keepdims=True)
            weighted = weighted + weigh(far_value, far_weights)
        weighted = weighted * (1.0 / total)
        own_acc[s] = weighted
        stat_out[s] = jnp.concatenate([top, total], axis=0)
        part = weighted.astype(bf16)
        for axis in axes:
            slot = s + LAG
            if slot < heads:
                block = early(slot, axis)
            for tile in range(blocks):
                piece = part[:, tile * TILE : (tile + 1) * TILE]
                if slot < heads:
                    cut = slice(tile * TILE, (tile + 1) * TILE)
                    piece = jnp.where(is_beside[cut], piece, block[cut])
                slot_out[slot, axis, tile] = piece
        for axis in axes:
            stats[s, axis] = remote(
                stat_out.at[s],
                stat_in.at[s, axis],
                stat_send.at[s, axis],
                stat_recv.at[s, axis],
                axis,
            )
            send(slot, axis)

    def combine(i):
        for side in (0, 1):
            first, last = 2 * i + side, 2 * i + 1 - side
            sources = ((stat_out[first], own_acc[first]),)
            for s, axis in ((first, 1), (last, 0)):
                block = jnp.concatenate(
                    [slot_in[s + LAG, axis, tile] for tile in range(blocks)], axis=1
                )
                sources += ((stat_in[s, axis], block.astype(f32)),)
            top = functools.reduce(jnp.maximum, [stat[0:1] for stat, _ in sources])
            sums = [stat[1:2] * jnp.exp2((stat[0:1] - top) * scale) for stat, _ in sources]
            inverse = 1.0 / functools.reduce(jnp.add, sums)
            attended = functools.reduce(
                jnp.add, [part * (total * inverse) for total, (_, part) in zip(sums, sources)]
            )
            att_buf[i, :, side * width : (side + 1) * width] = attended.T.astype(bf16)

    chunk = min(4 * TILE, features)

    def project(i):
        left = att_buf[i]

        def body(n, carry):
            cut = pl.ds(pl.multiple_of(n * chunk, chunk), chunk)
            product = jnp.dot(left, w_buf[i, :, cut], preferred_element_type=f32)
            if i == 0:
                update[:, cut] = state_buf[:, cut].astype(f32) + product
            else:
                update[:, cut] = update[:, cut] + product
            return carry

        lax.fori_loop(0, features // chunk, body, 0)

    for s in range(heads + LAG):
        for axis in axes:
            slots[s, axis].wait_recv()
            if s >= LAG:
                stats[s - LAG, axis].wait_recv()
        if s < heads:
            step(s)
        if s == LAG:
            for copy in w_copies:
                copy.wait()
            state_copy.wait()
            gain_copy.wait()
        if s > LAG and (s - LAG) % 2 == 1:
            i = (s - LAG) // 2
            combine(i)
            if i < half - 1:
                project(i)

    gain = gain_buf[...].astype(f32).reshape(1, -1)
    i = half - 1
    for block in range(blocks):
        cut = slice(block * TILE, (block + 1) * TILE)
        product = jnp.dot(att_buf[i, cut, :], w_buf[i], preferred_element_type=f32)
        mixed = update[cut, :] + product
        mean = jnp.mean(mixed * mixed, axis=-1, keepdims=True)
        normed = mixed * lax.rsqrt(mean + 1e-06) * gain
        active = jnp.full(normed.shape, halt[block * TILE] > STEP)
        kept = state_buf[cut, :].astype(f32)
        out_ref[cut, :] = jnp.where(active, normed, kept).astype(out_ref.dtype)

    for copy in copies:
        copy.wait_send()


def on_star(state_rows, q, k, v, halt_counts, out_weight, norm_gain):
    heads, rows, width = q.shape
    features = state_rows.shape[1]
    half, blocks, slots = heads // 2, rows // TILE, heads + LAG
    bf16, f32 = jnp.bfloat16, jnp.float32
    hbm = pl.BlockSpec(memory_space=pltpu.MemorySpace.HBM)
    vmem = pl.BlockSpec(memory_space=pltpu.VMEM)
    dma = pltpu.SemaphoreType.DMA
    operands = (halt_counts, q, k, v, state_rows, out_weight, norm_gain)
    return pl.pallas_call(
        star_kernel,
        out_shape=jax.ShapeDtypeStruct((rows, features), bf16),
        in_specs=[hbm] * len(operands),
        out_specs=vmem,
        scratch_shapes=[
            pltpu.SMEM((rows,), jnp.int32),
            pltpu.VMEM((features,), bf16),
            pltpu.VMEM((8, width), f32),
            pltpu.VMEM((2, 8, width), f32),
            pltpu.VMEM((heads, rows, width), bf16),
            pltpu.VMEM((heads, rows, width), bf16),
            pltpu.VMEM((heads, rows, width), bf16),
            pltpu.VMEM((slots, 2, blocks, TILE, width), bf16),
            pltpu.VMEM((slots, 2, blocks, TILE, width), bf16),
            pltpu.VMEM((heads, 2, rows), f32),
            pltpu.VMEM((heads, 2, 2, rows), f32),
            pltpu.VMEM((heads, width, rows), f32),
            pltpu.VMEM((half, rows, 2 * width), bf16),
            pltpu.VMEM((rows, features), bf16),
            pltpu.VMEM((half, 2 * width, features), bf16),
            pltpu.VMEM((rows, features), f32),
            dma,
            dma,
            dma,
            dma((3, heads)),
            dma((half, 2)),
            dma((2,)),
            dma((2,)),
            dma((slots, 2)),
            dma((slots, 2)),
            dma((heads, 2)),
            dma((heads, 2)),
        ],
        compiler_params=pltpu.CompilerParams(
            collective_id=0, has_side_effects=True, vmem_limit_bytes=32 * 1024 * 1024
        ),
    )(*[pltpu.with_memory_space_constraint(x, pltpu.HBM) for x in operands])


def fold_heads(carry, queries, key_piece, value_piece, score_scale):
    running_max, running_sum, weighted = carry

    def per_head(head_items):
        query_head, key_head, value_head, max_head, sum_head, weighted_head = head_items
        scores = (
            lax.dot_general(
                query_head, key_head, (((1,), (1,)), ((), ())), preferred_element_type=jnp.float32
            )
            * score_scale
        )
        new_max = jnp.maximum(max_head, jnp.max(scores, axis=1))
        shrink = jnp.exp(max_head - new_max)
        exponents = jnp.exp(scores - new_max[:, None])
        sum_head = sum_head * shrink + jnp.sum(exponents, axis=1)
        weighted_head = weighted_head * shrink[:, None] + jnp.dot(
            exponents.astype(jnp.bfloat16), value_head, preferred_element_type=jnp.float32
        )
        return (new_max, sum_head, weighted_head)

    return lax.map(per_head, (queries, key_piece, value_piece, running_max, running_sum, weighted))


def empty_carry(head_count, query_count, head_width):
    return (
        jnp.full((head_count, query_count), -1e30, jnp.float32),
        jnp.zeros((head_count, query_count), jnp.float32),
        jnp.zeros((head_count, query_count, head_width), jnp.float32),
    )


def attend_keys(query_vectors, key_vectors, value_vectors, score_scale):
    head_count, row_count, head_width = query_vectors.shape
    initial = empty_carry(head_count, row_count, head_width)
    running_max, running_sum, weighted = fold_heads(
        initial,
        query_vectors,
        lax.all_gather(key_vectors, "ctx", axis=1, tiled=True),
        lax.all_gather(value_vectors, "ctx", axis=1, tiled=True),
        score_scale,
    )
    return (weighted / running_sum[..., None]).astype(jnp.bfloat16)


def on_device(
    state_rows, query_vectors, key_vectors, value_vectors, halt_counts, out_weight, norm_gain
):
    head_count, row_count, head_width = query_vectors.shape
    score_scale = head_width ** (-0.5)
    attended = attend_keys(query_vectors, key_vectors, value_vectors, score_scale)
    update = jnp.einsum("hqd,hde->qe", attended, out_weight, preferred_element_type=jnp.float32)
    mixed_sum = state_rows.astype(jnp.float32) + update
    normed = (
        mixed_sum
        * lax.rsqrt(jnp.mean(mixed_sum * mixed_sum, axis=-1, keepdims=True) + 1e-06)
        * norm_gain.astype(jnp.float32)
    )
    active = (halt_counts > STEP)[:, None]
    return jnp.where(active, normed.astype(jnp.bfloat16), state_rows)


def solution(mesh):
    n_ctx = mesh.shape["ctx"]

    def per_device(state_rows, q, k, v, halt_counts, out_weight, norm_gain):
        heads, rows, width = q.shape
        one_owner = rows == (n_ctx - 1) * TILE
        if one_owner and heads % 2 == 0 and heads > LAG and width == TILE and n_ctx == 4:
            return on_star(state_rows, q, k, v, halt_counts, out_weight, norm_gain)
        return on_device(state_rows, q, k, v, halt_counts, out_weight, norm_gain)

    placed = (
        P(("dp", "ctx"), None),
        P(None, ("dp", "ctx"), None),
        P(None, ("dp", "ctx"), None),
        P(None, ("dp", "ctx"), None),
        P(("dp", "ctx")),
        P(),
        P(),
    )
    return jax.shard_map(
        per_device, mesh=mesh, in_specs=placed, out_specs=P(("dp", "ctx"), None), check_vma=False
    )
```

time: 35.4 us -> 32.5 us (0.918)
  Pallas kernels: 34.1 us -> 31.2 us
    pallas_call x1, Pallas kernels: 34.1 us -> 31.2 us  [on_star(): pl.pallas_call(star_kernel, out_shape=jax.ShapeDtypeStruct((rows, feature...]
where the time goes in v3:
time: 32.5 us; the launch traced here: 32.4 us
  Pallas kernels  31.2 us (96%)
  local copies, waits for them, and re-layouts  1.15 us (4%)
    pallas_call x1, Pallas kernels, on_star(): pl.pallas_call(star_kernel, out_shape=jax.ShapeDtypeStruct((rows, feature...  31.2 us
    unnamed x1, local copies, waits for them, and re-layouts  1.15 us

profile of v3, /device:TPU:0, one launch (start us, length us, event | category | flops | bytes accessed | tf_op | source)
XLA Modules:
  0.0 32.4 jit_solution(16395158370186349910)
XLA Ops:
  0.0 31.2 %shard_map.73 = bf16[384,2048]{1,0:T(8,128)(2,1)S(1)} custom-call(s32[384]{0:T(512)} %halt_hbm.1, bf16[8,384,128]{2,1,0:T(8,128)(2,1)} %q_hbm.1, bf16[8,384,128]{2,1,0:T(8,128)(2,1)} %k_hbm.1, bf16[8,384,128]{2,1,0:T(8,128)(2,1)} %v_hbm.1, bf16[384,2048]{1,0:T(8,128)(2,1)} %state_hbm.1, bf16[8,128,2048]{2,1,0:T(8,128)(2,1)} %w_hbm.1, bf16[2048]{0:T(1024)(128)(2,1)} %gain_hbm.1), custom_call_target="tpu_custom_call" | custom-call | tf_op jit(solution)/shard_map/pallas_call | solution.py:304
  31.2 1.1 %copy.9 = bf16[384,2048]{1,0:T(8,128)(2,1)} copy(bf16[384,2048]{1,0:T(8,128)(2,1)S(1)} %shard_map.73) | data formatting | bytes 3145728

commit v4 on v3

v4 whole, which is shorter than its diff:
```python
import functools

import jax
import jax.numpy as jnp
from jax import lax
from jax.experimental import pallas as pl
from jax.experimental.pallas import tpu as pltpu
from jax.sharding import PartitionSpec as P

STEP = 2
TILE = 128
LAG = 3
SLOTS = 3 * LAG + 1
LOG2E = 1.4426950408889634


def slot_orders(heads):
    half = heads // 2
    first = [half]
    singles = [heads - 1, 0]
    for j in range(half - 1):
        first += [j + 1] + singles[j : j + 1]
    return first, [(h + half) % heads for h in first]


def star_kernel(
    halt_hbm,
    q_hbm,
    k_hbm,
    v_hbm,
    state_hbm,
    w_hbm,
    gain_hbm,
    out_ref,
    halt,
    gain_buf,
    flag_out,
    flag_in,
    qkv_buf,
    slot_out,
    slot_in,
    stat_out,
    stat_in,
    own_part,
    own_stat,
    att_buf,
    state_buf,
    w_buf,
    update,
    halt_sem,
    gain_sem,
    state_sem,
    w_sem,
    flag_send,
    flag_recv,
    slot_send,
    stat_send,
    qkv_sem,
    slot_recv,
    stat_recv,
):
    me = lax.axis_index("ctx")
    bits = (me % 2, me // 2)
    peer = (bits[1] * 2 + 1 - bits[0], (1 - bits[1]) * 2 + bits[0])
    heads, rows, width = q_hbm.shape
    features = state_hbm.shape[1]
    half = heads // 2
    early = heads - 2
    blocks = rows // TILE
    scale = width ** (-0.5) * LOG2E
    axes = (0, 1)
    orders = slot_orders(heads)
    f32, bf16 = jnp.float32, jnp.bfloat16

    def local(src, dst, sem):
        copy = pltpu.make_async_copy(src, dst, sem)
        copy.start()
        return copy

    def remote(src, dst, send, recv, axis):
        return pltpu.make_async_remote_copy(
            src_ref=src,
            dst_ref=dst,
            send_sem=send,
            recv_sem=recv,
            device_id={"ctx": peer[axis]},
            device_id_type=pl.DeviceIdType.MESH,
        )

    halt_copy = local(halt_hbm, halt, halt_sem)
    for i in range(half):
        for side in (0, 1):
            for n, operand in enumerate((q_hbm, k_hbm, v_hbm)):
                local(operand.at[side * half + i], qkv_buf.at[i, side, n], qkv_sem.at[i])
    loaded = set()

    def own(n, h):
        i = h % half
        if i not in loaded:
            pltpu.make_async_copy(qkv_buf.at[i], qkv_buf.at[i], qkv_sem.at[i]).wait()
            loaded.add(i)
        return qkv_buf[i, h // half, n]

    barrier = pltpu.get_barrier_semaphore()
    for axis in axes:
        pl.semaphore_signal(
            barrier, inc=1, device_id={"ctx": peer[axis]}, device_id_type=pl.DeviceIdType.MESH
        )
    halt_copy.wait()
    flag = jnp.full(flag_out.shape, halt[0] > STEP).astype(f32)
    flag_out[...] = flag

    def mask(value):
        return jnp.broadcast_to(value[0:1, :].astype(bf16), (rows, width)) > 0.5

    is_owner = mask(flag)

    def opening(s, axis):
        other = orders[1 - axis][2 * (s // 2) + 1]
        return jnp.where(is_owner, own(0, orders[axis][s]), own(1 + s % 2, other))

    def send(s):
        for axis in axes:
            remote(
                slot_out.at[s, axis], slot_in.at[s, axis], slot_send, slot_recv.at[s], axis
            ).start()

    for s in range(LAG):
        for axis in axes:
            slot_out[s, axis] = opening(s, axis).reshape(blocks, TILE, width)
        if s == 0:
            pl.semaphore_wait(barrier, 2)
            for axis in axes:
                remote(flag_out, flag_in.at[axis], flag_send.at[axis], flag_recv, axis).start()
        send(s)

    for side in (0, 1):
        local(
            w_hbm.at[pl.ds(side * half, half)], w_buf.at[:, pl.ds(side * width, width)], w_sem
        )
    state_copy = local(state_hbm, state_buf, state_sem)
    gain_copy = local(gain_hbm, gain_buf, gain_sem)

    remote(flag_in, flag_in, flag_send.at[0], flag_recv, 0).wait_recv()
    owner_at = [mask(flag_in[axis]) for axis in axes]
    beside = flag_in[0] + flag_in[1]
    is_beside = mask(beside)

    def bias(valid):
        return jnp.concatenate([(valid[0:1, :] - 1.0) * 1e30] * blocks, axis=1)

    def received(s, axis):
        return slot_in[s, axis].reshape(rows, width)

    def attend(query, keys, values):
        scores = lax.dot_general(
            keys, query, (((1,), (1,)), ((), ())), preferred_element_type=f32
        )
        top = jnp.max(scores, axis=0, keepdims=True)
        weights = jnp.exp2((scores - top) * scale)
        total = jnp.sum(weights, axis=0, keepdims=True)
        weighted = lax.dot_general(
            values, weights.astype(bf16), (((0,), (0,)), ((), ())), preferred_element_type=f32
        )
        return top, total, weighted * (1.0 / total)

    def merge(sources):
        top = functools.reduce(jnp.maximum, [source[0] for source in sources])
        sums = [total * jnp.exp2((source - top) * scale) for source, total, _ in sources]
        total = functools.reduce(jnp.add, sums)
        inverse = 1.0 / total
        parts = [part * (each * inverse) for each, (_, _, part) in zip(sums, sources)]
        return top, total, functools.reduce(jnp.add, parts)

    def put(s, results):
        for axis in axes:
            top, total, part = results[axis]
            part = part.astype(bf16)
            stat_out[s - LAG - 1, axis] = jnp.concatenate([top, total], axis=0)
            block = opening(s, axis) if s < early else None
            for tile in range(blocks):
                cut = slice(tile * TILE, (tile + 1) * TILE)
                piece = part[:, cut]
                if s < early:
                    piece = jnp.where(is_beside[cut], piece, block[cut])
                slot_out[s, axis, tile] = piece
            remote(
                stat_out.at[s - LAG - 1, axis],
                stat_in.at[s - LAG - 1, axis],
                stat_send,
                stat_recv.at[s - LAG - 1],
                axis,
            ).start()
        send(s)

    def keep(h, result):
        own_stat[h] = jnp.concatenate(result[:2], axis=0)
        own_part[h] = result[2]

    def kept(h):
        return own_stat[h, 0:1], own_stat[h, 1:2], own_part[h]

    def sent(s, axis):
        block = jnp.concatenate([slot_in[s, axis, tile] for tile in range(blocks)], axis=1)
        stat = stat_in[s - LAG - 1, axis]
        return stat[0:1], stat[1:2], block.astype(f32)

    def select(value, first, second):
        line = jnp.concatenate([value[0:1, :]] * blocks, axis=1)
        return tuple(
            jnp.where(jnp.broadcast_to(line, a.shape) > 0.5, a, b) for a, b in zip(first, second)
        )

    def step(s):
        high, low = orders[0][s], orders[1][s]
        query = jnp.where(
            owner_at[0], received(s, 0), jnp.where(owner_at[1], received(s, 1), own(0, low))
        )
        key = jnp.where(owner_at[0], own(1, high), own(1, low))
        value = jnp.where(owner_at[0], own(2, high), own(2, low))
        if s % 2 == 0:
            result = attend(query, key, value)
            keep(low, result)
            if s > 0:
                put(s + LAG, (result, result))
            else:
                for axis in axes:
                    block = jnp.where(owner_at[1 - axis], query, opening(LAG, axis))
                    slot_out[LAG, axis] = block.reshape(blocks, TILE, width)
                send(LAG)
            return
        far_key = jnp.where(owner_at[0], received(s - 1, 1), received(s - 1, 0))
        far_value = jnp.where(owner_at[0], received(s, 1), received(s, 0))
        far_query = query
        valid = beside if s > LAG else beside + flag
        if s == LAG:
            far, near = orders[0][0], orders[1][0]
            take = mask(flag + beside)
            query = jnp.where(take, query, received(s, 1))
            key = jnp.where(take, key, own(1, far))
            value = jnp.where(take, value, own(2, far))
            far_query = jnp.where(take, far_query, received(s, 0))
            far_key = jnp.where(take, far_key, own(1, near))
            far_value = jnp.where(take, far_value, own(2, near))
        nearby = attend(query, key, value)
        distant = attend(far_query, far_key, far_value)
        result = merge((nearby, (distant[0] + bias(valid),) + distant[1:]))
        keep(low, result)
        if s == LAG:
            put(
                s + LAG,
                (select(beside, result, distant), select(beside, result, nearby)),
            )
        else:
            put(s + LAG, (result, result))
        if s <= LAG:
            nearby = attend(own(0, high), own(1, high), own(2, high))
            distant = attend(own(0, high), received(s - 1, 1), received(s, 1))
            keep(high, merge((nearby, distant)))

    def finish_first():
        near, far = orders[1][0], 2 * LAG
        result = merge((kept(near), select(flag_in[0], sent(far, 1), sent(far, 0))))
        put(SLOTS - 1, (result, result))

    def combine(i):
        for side in (0, 1):
            h = i + side * half
            sources = [kept(h)]
            for axis in axes:
                if h in orders[axis]:
                    s = orders[axis].index(h)
                    sources.append(sent(s + LAG if s > 0 else SLOTS - 1, axis))
            attended = merge(sources)[2]
            att_buf[i, :, side * width : (side + 1) * width] = attended.T.astype(bf16)

    chunk = min(4 * TILE, features)

    def project(i, initial):
        left = att_buf[i]

        def body(n, carry):
            cut = pl.ds(pl.multiple_of(n * chunk, chunk), chunk)
            product = jnp.dot(left, w_buf[i, :, cut], preferred_element_type=f32)
            if initial:
                update[:, cut] = state_buf[:, cut].astype(f32) + product
            else:
                update[:, cut] = update[:, cut] + product
            return carry

        lax.fori_loop(0, features // chunk, body, 0)

    for s in range(SLOTS):
        remote(slot_in.at[s], slot_in.at[s], slot_send, slot_recv.at[s], 0).wait_recv()
        if s > LAG:
            stat = s - LAG - 1
            remote(
                stat_in.at[stat], stat_in.at[stat], stat_send, stat_recv.at[stat], 0
            ).wait_recv()
        if s < early:
            step(s)
        elif s == early:
            finish_first()
        if s > LAG and s % 2 == 0:
            i = s // 2 - 1
            if i == 1:
                pltpu.make_async_copy(w_buf, w_buf, w_sem).wait()
                state_copy.wait()
                gain_copy.wait()
            combine(i)
            project(i, i == 1)
    combine(0)

    gain = gain_buf[...].astype(f32).reshape(1, -1)
    for block in range(blocks):
        cut = slice(block * TILE, (block + 1) * TILE)
        product = jnp.dot(att_buf[0, cut, :], w_buf[0], preferred_element_type=f32)
        mixed = update[cut, :] + product
        mean = jnp.mean(mixed * mixed, axis=-1, keepdims=True)
        normed = mixed * lax.rsqrt(mean + 1e-06) * gain
        active = jnp.full(normed.shape, halt[block * TILE] > STEP)
        unchanged = state_buf[cut, :].astype(f32)
        out_ref[cut, :] = jnp.where(active, normed, unchanged).astype(out_ref.dtype)

    remote(slot_out, slot_in, slot_send, slot_recv.at[0], 0).wait_send()
    remote(stat_out, stat_in, stat_send, stat_recv.at[0], 0).wait_send()
    for axis in axes:
        remote(flag_out, flag_in.at[axis], flag_send.at[axis], flag_recv, axis).wait_send()


def on_star(state_rows, q, k, v, halt_counts, out_weight, norm_gain):
    heads, rows, width = q.shape
    features = state_rows.shape[1]
    half, blocks, stats = heads // 2, rows // TILE, SLOTS - LAG - 1
    bf16, f32 = jnp.bfloat16, jnp.float32
    hbm = pl.BlockSpec(memory_space=pltpu.MemorySpace.HBM)
    vmem = pl.BlockSpec(memory_space=pltpu.VMEM)
    dma = pltpu.SemaphoreType.DMA
    operands = (halt_counts, q, k, v, state_rows, out_weight, norm_gain)
    return pl.pallas_call(
        star_kernel,
        out_shape=jax.ShapeDtypeStruct((rows, features), bf16),
        in_specs=[hbm] * len(operands),
        out_specs=vmem,
        scratch_shapes=[
            pltpu.SMEM((rows,), jnp.int32),
            pltpu.VMEM((features,), bf16),
            pltpu.VMEM((8, width), f32),
            pltpu.VMEM((2, 8, width), f32),
            pltpu.VMEM((half, 2, 3, rows, width), bf16),
            pltpu.VMEM((SLOTS, 2, blocks, TILE, width), bf16),
            pltpu.VMEM((SLOTS, 2, blocks, TILE, width), bf16),
            pltpu.VMEM((stats, 2, 2, rows), f32),
            pltpu.VMEM((stats, 2, 2, rows), f32),
            pltpu.VMEM((heads, width, rows), f32),
            pltpu.VMEM((heads, 2, rows), f32),
            pltpu.VMEM((half, rows, 2 * width), bf16),
            pltpu.VMEM((rows, features), bf16),
            pltpu.VMEM((half, 2 * width, features), bf16),
            pltpu.VMEM((rows, features), f32),
            dma,
            dma,
            dma,
            dma,
            dma((2,)),
            dma,
            dma,
            dma,
            dma((half,)),
            dma((SLOTS,)),
            dma((stats,)),
        ],
        compiler_params=pltpu.CompilerParams(
            collective_id=0, has_side_effects=True, vmem_limit_bytes=32 * 1024 * 1024
        ),
    )(*[pltpu.with_memory_space_constraint(x, pltpu.HBM) for x in operands])


def fold_heads(carry, queries, key_piece, value_piece, score_scale):
    running_max, running_sum, weighted = carry

    def per_head(head_items):
        query_head, key_head, value_head, max_head, sum_head, weighted_head = head_items
        scores = (
            lax.dot_general(
                query_head, key_head, (((1,), (1,)), ((), ())), preferred_element_type=jnp.float32
            )
            * score_scale
        )
        new_max = jnp.maximum(max_head, jnp.max(scores, axis=1))
        shrink = jnp.exp(max_head - new_max)
        exponents = jnp.exp(scores - new_max[:, None])
        sum_head = sum_head * shrink + jnp.sum(exponents, axis=1)
        weighted_head = weighted_head * shrink[:, None] + jnp.dot(
            exponents.astype(jnp.bfloat16), value_head, preferred_element_type=jnp.float32
        )
        return (new_max, sum_head, weighted_head)

    return lax.map(per_head, (queries, key_piece, value_piece, running_max, running_sum, weighted))


def empty_carry(head_count, query_count, head_width):
    return (
        jnp.full((head_count, query_count), -1e30, jnp.float32),
        jnp.zeros((head_count, query_count), jnp.float32),
        jnp.zeros((head_count, query_count, head_width), jnp.float32),
    )


def attend_keys(query_vectors, key_vectors, value_vectors, score_scale):
    head_count, row_count, head_width = query_vectors.shape
    initial = empty_carry(head_count, row_count, head_width)
    running_max, running_sum, weighted = fold_heads(
        initial,
        query_vectors,
        lax.all_gather(key_vectors, "ctx", axis=1, tiled=True),
        lax.all_gather(value_vectors, "ctx", axis=1, tiled=True),
        score_scale,
    )
    return (weighted / running_sum[..., None]).astype(jnp.bfloat16)


def on_device(
    state_rows, query_vectors, key_vectors, value_vectors, halt_counts, out_weight, norm_gain
):
    head_count, row_count, head_width = query_vectors.shape
    score_scale = head_width ** (-0.5)
    attended = attend_keys(query_vectors, key_vectors, value_vectors, score_scale)
    update = jnp.einsum("hqd,hde->qe", attended, out_weight, preferred_element_type=jnp.float32)
    mixed_sum = state_rows.astype(jnp.float32) + update
    normed = (
        mixed_sum
        * lax.rsqrt(jnp.mean(mixed_sum * mixed_sum, axis=-1, keepdims=True) + 1e-06)
        * norm_gain.astype(jnp.float32)
    )
    active = (halt_counts > STEP)[:, None]
    return jnp.where(active, normed.astype(jnp.bfloat16), state_rows)


def solution(mesh):
    n_ctx = mesh.shape["ctx"]

    def per_device(state_rows, q, k, v, halt_counts, out_weight, norm_gain):
        heads, rows, width = q.shape
        one_owner = rows == (n_ctx - 1) * TILE
        if one_owner and heads - 2 == 2 * LAG and width == TILE and n_ctx == 4:
            return on_star(state_rows, q, k, v, halt_counts, out_weight, norm_gain)
        return on_device(state_rows, q, k, v, halt_counts, out_weight, norm_gain)

    placed = (
        P(("dp", "ctx"), None),
        P(None, ("dp", "ctx"), None),
        P(None, ("dp", "ctx"), None),
        P(None, ("dp", "ctx"), None),
        P(("dp", "ctx")),
        P(),
        P(),
    )
    return jax.shard_map(
        per_device, mesh=mesh, in_specs=placed, out_specs=P(("dp", "ctx"), None), check_vma=False
    )
```

time: 32.5 us -> 29.7 us (0.914)
  Pallas kernels: 31.2 us -> 28.4 us
    pallas_call x1, Pallas kernels: 31.2 us -> 28.4 us  [on_star(): pl.pallas_call(star_kernel, out_shape=jax.ShapeDtypeStruct((rows, feature...]
where the time goes in v4:
time: 29.7 us; the launch traced here: 29.6 us
  Pallas kernels  28.4 us (96%)
  local copies, waits for them, and re-layouts  1.15 us (4%)
    pallas_call x1, Pallas kernels, on_star(): pl.pallas_call(star_kernel, out_shape=jax.ShapeDtypeStruct((rows, feature...  28.4 us
    unnamed x1, local copies, waits for them, and re-layouts  1.15 us

profile of v4, /device:TPU:0, one launch (start us, length us, event | category | flops | bytes accessed | tf_op | source)
XLA Modules:
  0.0 29.6 jit_solution(17284988281130346272)
XLA Ops:
  0.0 28.4 %shard_map.73 = bf16[384,2048]{1,0:T(8,128)(2,1)S(1)} custom-call(s32[384]{0:T(512)} %halt_hbm.1, bf16[8,384,128]{2,1,0:T(8,128)(2,1)} %q_hbm.1, bf16[8,384,128]{2,1,0:T(8,128)(2,1)} %k_hbm.1, bf16[8,384,128]{2,1,0:T(8,128)(2,1)} %v_hbm.1, bf16[384,2048]{1,0:T(8,128)(2,1)} %state_hbm.1, bf16[8,128,2048]{2,1,0:T(8,128)(2,1)} %w_hbm.1, bf16[2048]{0:T(1024)(128)(2,1)} %gain_hbm.1), custom_call_target="tpu_custom_call" | custom-call | tf_op jit(solution)/shard_map/pallas_call | solution.py:340
  28.4 1.1 %copy.9 = bf16[384,2048]{1,0:T(8,128)(2,1)} copy(bf16[384,2048]{1,0:T(8,128)(2,1)S(1)} %shard_map.73) | data formatting | bytes 3145728

commit v5 on v4

--- a/solution.py
+++ b/solution.py
@@ -57,6 +57,7 @@
     stat_send,
     qkv_sem,
     slot_recv,
+    tile_recv,
     stat_recv,
 ):
     me = lax.axis_index("ctx")
@@ -87,25 +88,35 @@
             device_id_type=pl.DeviceIdType.MESH,
         )
 
-    halt_copy = local(halt_hbm, halt, halt_sem)
-    for i in range(half):
-        for side in (0, 1):
-            for n, operand in enumerate((q_hbm, k_hbm, v_hbm)):
-                local(operand.at[side * half + i], qkv_buf.at[i, side, n], qkv_sem.at[i])
-    loaded = set()
-
-    def own(n, h):
-        i = h % half
-        if i not in loaded:
-            pltpu.make_async_copy(qkv_buf.at[i], qkv_buf.at[i], qkv_sem.at[i]).wait()
-            loaded.add(i)
-        return qkv_buf[i, h // half, n]
-
     barrier = pltpu.get_barrier_semaphore()
     for axis in axes:
         pl.semaphore_signal(
             barrier, inc=1, device_id={"ctx": peer[axis]}, device_id_type=pl.DeviceIdType.MESH
         )
+    halt_copy = local(halt_hbm, halt, halt_sem)
+
+    def choices(s, axis):
+        return (0, orders[axis][s]), (1 + s % 2, orders[1 - axis][2 * (s // 2) + 1])
+
+    group_of = {}
+    for s in range(LAG):
+        for axis in axes:
+            for block in choices(s, axis):
+                group_of[block] = min(s, 1)
+    for block in [(n, h) for h in range(heads) for n in range(3)]:
+        group_of.setdefault(block, 2)
+    for (n, h), group in group_of.items():
+        local((q_hbm, k_hbm, v_hbm)[n].at[h], qkv_buf.at[n * heads + h], qkv_sem.at[group])
+    loaded = set()
+
+    def own(n, h):
+        group = group_of[n, h]
+        if group not in loaded:
+            whole = qkv_buf.at[pl.ds(0, list(group_of.values()).count(group))]
+            pltpu.make_async_copy(whole, whole, qkv_sem.at[group]).wait()
+            loaded.add(group)
+        return qkv_buf[n * heads + h]
+
     halt_copy.wait()
     flag = jnp.full(flag_out.shape, halt[0] > STEP).astype(f32)
     flag_out[...] = flag
@@ -116,14 +127,35 @@
     is_owner = mask(flag)
 
     def opening(s, axis):
-        other = orders[1 - axis][2 * (s // 2) + 1]
-        return jnp.where(is_owner, own(0, orders[axis][s]), own(1 + s % 2, other))
+        mine, other = choices(s, axis)
+        return jnp.where(is_owner, own(*mine), own(*other))
 
     def send(s):
-        for axis in axes:
-            remote(
-                slot_out.at[s, axis], slot_in.at[s, axis], slot_send, slot_recv.at[s], axis
-            ).start()
+        if s < SLOTS - 2:
+            for axis in axes:
+                remote(
+                    slot_out.at[s, axis], slot_in.at[s, axis], slot_send, slot_recv.at[s], axis
+                ).start()
+            return
+        for tile in range(blocks):
+            for axis in axes:
+                remote(
+                    slot_out.at[s, axis, tile],
+                    slot_in.at[s, axis, tile],
+                    slot_send,
+                    tile_recv.at[s - SLOTS + 2, tile],
+                    axis,
+                ).start()
+
+    def wait_tile(s, tile):
+        landed = slot_in.at[s, pl.ds(0, 2), tile]
+        remote(landed, landed, slot_send, tile_recv.at[s - SLOTS + 2, tile], 0).wait_recv()
+
+    def wait_stat(s):
+        stat = s - LAG - 1
+        remote(
+            stat_in.at[stat], stat_in.at[stat], stat_send, stat_recv.at[stat], 0
+        ).wait_recv()
 
     for s in range(LAG):
         for axis in axes:
@@ -197,13 +229,18 @@
         own_stat[h] = jnp.concatenate(result[:2], axis=0)
         own_part[h] = result[2]
 
-    def kept(h):
-        return own_stat[h, 0:1], own_stat[h, 1:2], own_part[h]
-
-    def sent(s, axis):
-        block = jnp.concatenate([slot_in[s, axis, tile] for tile in range(blocks)], axis=1)
-        stat = stat_in[s - LAG - 1, axis]
-        return stat[0:1], stat[1:2], block.astype(f32)
+    def cut_of(tiles):
+        return slice(tiles[0] * TILE, (tiles[-1] + 1) * TILE)
+
+    def kept(h, tiles=range(blocks)):
+        cut = cut_of(tiles)
+        return own_stat[h, 0:1, cut], own_stat[h, 1:2, cut], own_part[h, :, cut]
+
+    def sent(s, axis, tiles=range(blocks)):
+        cut, stat = cut_of(tiles), s - LAG - 1
+        block = jnp.concatenate([slot_in[s, axis, tile] for tile in tiles], axis=1)
+        top, total = stat_in[stat, axis, 0:1, cut], stat_in[stat, axis, 1:2, cut]
+        return top, total, block.astype(f32)
 
     def select(value, first, second):
         line = jnp.concatenate([value[0:1, :]] * blocks, axis=1)
@@ -263,16 +300,16 @@
         result = merge((kept(near), select(flag_in[0], sent(far, 1), sent(far, 0))))
         put(SLOTS - 1, (result, result))
 
-    def combine(i):
+    def combine(i, tiles=range(blocks)):
         for side in (0, 1):
             h = i + side * half
-            sources = [kept(h)]
+            sources = [kept(h, tiles)]
             for axis in axes:
                 if h in orders[axis]:
                     s = orders[axis].index(h)
-                    sources.append(sent(s + LAG if s > 0 else SLOTS - 1, axis))
+                    sources.append(sent(s + LAG if s > 0 else SLOTS - 1, axis, tiles))
             attended = merge(sources)[2]
-            att_buf[i, :, side * width : (side + 1) * width] = attended.T.astype(bf16)
+            att_buf[i, cut_of(tiles), side * width : (side + 1) * width] = attended.T.astype(bf16)
 
     chunk = min(4 * TILE, features)
 
@@ -290,13 +327,10 @@
 
         lax.fori_loop(0, features // chunk, body, 0)
 
-    for s in range(SLOTS):
+    for s in range(SLOTS - 2):
         remote(slot_in.at[s], slot_in.at[s], slot_send, slot_recv.at[s], 0).wait_recv()
         if s > LAG:
-            stat = s - LAG - 1
-            remote(
-                stat_in.at[stat], stat_in.at[stat], stat_send, stat_recv.at[stat], 0
-            ).wait_recv()
+            wait_stat(s)
         if s < early:
             step(s)
         elif s == early:
@@ -309,18 +343,42 @@
                 gain_copy.wait()
             combine(i)
             project(i, i == 1)
-    combine(0)
-
-    gain = gain_buf[...].astype(f32).reshape(1, -1)
-    for block in range(blocks):
-        cut = slice(block * TILE, (block + 1) * TILE)
-        product = jnp.dot(att_buf[0, cut, :], w_buf[0], preferred_element_type=f32)
-        mixed = update[cut, :] + product
-        mean = jnp.mean(mixed * mixed, axis=-1, keepdims=True)
-        normed = mixed * lax.rsqrt(mean + 1e-06) * gain
-        active = jnp.full(normed.shape, halt[block * TILE] > STEP)
-        unchanged = state_buf[cut, :].astype(f32)
-        out_ref[cut, :] = jnp.where(active, normed, unchanged).astype(out_ref.dtype)
+
+    strips = [slice(n, n + 2 * TILE) for n in range(0, features, 2 * TILE)]
+
+    def add_product(i, tiles):
+        cut = cut_of(tiles)
+        left = att_buf[i, cut, :]
+        squares = jnp.zeros((len(tiles) * TILE, TILE), f32)
+        for strip in strips:
+            mixed = update[cut, strip] + jnp.dot(
+                left, w_buf[i, :, strip], preferred_element_type=f32
+            )
+            update[cut, strip] = mixed
+            squares = squares + mixed[:, :TILE] * mixed[:, :TILE]
+            squares = squares + mixed[:, TILE:] * mixed[:, TILE:]
+        return squares
+
+    wait_stat(SLOTS - 2)
+    for tile in range(blocks):
+        wait_tile(SLOTS - 2, tile)
+        combine(half - 1, [tile])
+        add_product(half - 1, [tile])
+
+    wait_stat(SLOTS - 1)
+    for tiles in ([0], list(range(1, blocks))):
+        for tile in tiles:
+            wait_tile(SLOTS - 1, tile)
+        combine(0, tiles)
+        squares = add_product(0, tiles)
+        inverse = lax.rsqrt(jnp.sum(squares, axis=-1, keepdims=True) / features + 1e-06)
+        for strip in strips:
+            gain = gain_buf[strip].astype(f32).reshape(1, -1)
+            for tile in tiles:
+                cut, own_cut = cut_of([tile]), cut_of([tile - tiles[0]])
+                active = jnp.full((TILE, 2 * TILE), halt[tile * TILE] > STEP).astype(bf16) > 0.5
+                normed = (update[cut, strip] * inverse[own_cut] * gain).astype(bf16)
+                out_ref[cut, strip] = jnp.where(active, normed, state_buf[cut, strip])
 
     remote(slot_out, slot_in, slot_send, slot_recv.at[0], 0).wait_send()
     remote(stat_out, stat_in, stat_send, stat_recv.at[0], 0).wait_send()
@@ -347,7 +405,7 @@
             pltpu.VMEM((features,), bf16),
             pltpu.VMEM((8, width), f32),
             pltpu.VMEM((2, 8, width), f32),
-            pltpu.VMEM((half, 2, 3, rows, width), bf16),
+            pltpu.VMEM((3 * heads, rows, width), bf16),
             pltpu.VMEM((SLOTS, 2, blocks, TILE, width), bf16),
             pltpu.VMEM((SLOTS, 2, blocks, TILE, width), bf16),
             pltpu.VMEM((stats, 2, 2, rows), f32),
@@ -366,8 +424,9 @@
             dma,
             dma,
             dma,
-            dma((half,)),
-            dma((SLOTS,)),
+            dma((3,)),
+            dma((SLOTS - 2,)),
+            dma((2, blocks)),
             dma((stats,)),
         ],
         compiler_params=pltpu.CompilerParams(

time: 29.7 us -> 28.9 us (0.973)
  Pallas kernels: 28.4 us -> 27.6 us
    pallas_call x1, Pallas kernels: 28.4 us -> 27.6 us  [on_star(): pl.pallas_call(star_kernel, out_shape=jax.ShapeDtypeStruct((rows, feature...]
where the time goes in v5:
time: 28.9 us; the launch traced here: 28.7 us
  Pallas kernels  27.6 us (96%)
  local copies, waits for them, and re-layouts  1.15 us (4%)
    pallas_call x1, Pallas kernels, on_star(): pl.pallas_call(star_kernel, out_shape=jax.ShapeDtypeStruct((rows, feature...  27.6 us
    unnamed x1, local copies, waits for them, and re-layouts  1.15 us

profile of v5, /device:TPU:0, one launch (start us, length us, event | category | flops | bytes accessed | tf_op | source)
XLA Modules:
  0.0 28.7 jit_solution(4150832305998454896)
XLA Ops:
  0.0 27.6 %shard_map.73 = bf16[384,2048]{1,0:T(8,128)(2,1)S(1)} custom-call(s32[384]{0:T(512)} %halt_hbm.1, bf16[8,384,128]{2,1,0:T(8,128)(2,1)} %q_hbm.1, bf16[8,384,128]{2,1,0:T(8,128)(2,1)} %k_hbm.1, bf16[8,384,128]{2,1,0:T(8,128)(2,1)} %v_hbm.1, bf16[384,2048]{1,0:T(8,128)(2,1)} %state_hbm.1, bf16[8,128,2048]{2,1,0:T(8,128)(2,1)} %w_hbm.1, bf16[2048]{0:T(1024)(128)(2,1)} %gain_hbm.1), custom_call_target="tpu_custom_call" | custom-call | tf_op jit(solution)/shard_map/pallas_call | solution.py:398
  27.6 1.1 %copy.9 = bf16[384,2048]{1,0:T(8,128)(2,1)} copy(bf16[384,2048]{1,0:T(8,128)(2,1)S(1)} %shard_map.73) | data formatting | bytes 3145728

commit v6 on v5

--- a/solution.py
+++ b/solution.py
@@ -31,9 +31,14 @@
     state_hbm,
     w_hbm,
     gain_hbm,
-    out_ref,
+    first_ref,
+    left_ref,
+    update,
+    w_last,
+    state_buf,
+    gain_buf,
+    active_ref,
     halt,
-    gain_buf,
     flag_out,
     flag_in,
     qkv_buf,
@@ -44,9 +49,7 @@
     own_part,
     own_stat,
     att_buf,
-    state_buf,
     w_buf,
-    update,
     halt_sem,
     gain_sem,
     state_sem,
@@ -167,9 +170,9 @@
         send(s)
 
     for side in (0, 1):
-        local(
-            w_hbm.at[pl.ds(side * half, half)], w_buf.at[:, pl.ds(side * width, width)], w_sem
-        )
+        cut = pl.ds(side * width, width)
+        local(w_hbm.at[pl.ds(side * half + 1, half - 1)], w_buf.at[:, cut], w_sem.at[0])
+        local(w_hbm.at[side * half], w_last.at[cut], w_sem.at[1])
     state_copy = local(state_hbm, state_buf, state_sem)
     gain_copy = local(gain_hbm, gain_buf, gain_sem)
 
@@ -194,21 +197,20 @@
         weighted = lax.dot_general(
             values, weights.astype(bf16), (((0,), (0,)), ((), ())), preferred_element_type=f32
         )
-        return top, total, weighted * (1.0 / total)
+        return top * scale + jnp.log2(total), weighted * (1.0 / total)
 
     def merge(sources):
-        top = functools.reduce(jnp.maximum, [source[0] for source in sources])
-        sums = [total * jnp.exp2((source - top) * scale) for source, total, _ in sources]
+        top = functools.reduce(jnp.maximum, [level for level, _ in sources])
+        sums = [jnp.exp2(level - top) for level, _ in sources]
         total = functools.reduce(jnp.add, sums)
         inverse = 1.0 / total
-        parts = [part * (each * inverse) for each, (_, _, part) in zip(sums, sources)]
-        return top, total, functools.reduce(jnp.add, parts)
+        parts = [part * (each * inverse) for each, (_, part) in zip(sums, sources)]
+        return top + jnp.log2(total), functools.reduce(jnp.add, parts)
 
     def put(s, results):
         for axis in axes:
-            top, total, part = results[axis]
+            stat_out[s - LAG - 1, axis], part = results[axis]
             part = part.astype(bf16)
-            stat_out[s - LAG - 1, axis] = jnp.concatenate([top, total], axis=0)
             block = opening(s, axis) if s < early else None
             for tile in range(blocks):
                 cut = slice(tile * TILE, (tile + 1) * TILE)
@@ -226,21 +228,19 @@
         send(s)
 
     def keep(h, result):
-        own_stat[h] = jnp.concatenate(result[:2], axis=0)
-        own_part[h] = result[2]
+        own_stat[h], own_part[h] = result
 
     def cut_of(tiles):
         return slice(tiles[0] * TILE, (tiles[-1] + 1) * TILE)
 
     def kept(h, tiles=range(blocks)):
         cut = cut_of(tiles)
-        return own_stat[h, 0:1, cut], own_stat[h, 1:2, cut], own_part[h, :, cut]
+        return own_stat[h, :, cut], own_part[h, :, cut]
 
     def sent(s, axis, tiles=range(blocks)):
         cut, stat = cut_of(tiles), s - LAG - 1
         block = jnp.concatenate([slot_in[s, axis, tile] for tile in tiles], axis=1)
-        top, total = stat_in[stat, axis, 0:1, cut], stat_in[stat, axis, 1:2, cut]
-        return top, total, block.astype(f32)
+        return stat_in[stat, axis, :, cut], block.astype(f32)
 
     def select(value, first, second):
         line = jnp.concatenate([value[0:1, :]] * blocks, axis=1)
@@ -281,7 +281,7 @@
             far_value = jnp.where(take, far_value, own(2, near))
         nearby = attend(query, key, value)
         distant = attend(far_query, far_key, far_value)
-        result = merge((nearby, (distant[0] + bias(valid),) + distant[1:]))
+        result = merge((nearby, (distant[0] + bias(valid), distant[1])))
         keep(low, result)
         if s == LAG:
             put(
@@ -308,7 +308,7 @@
                 if h in orders[axis]:
                     s = orders[axis].index(h)
                     sources.append(sent(s + LAG if s > 0 else SLOTS - 1, axis, tiles))
-            attended = merge(sources)[2]
+            attended = merge(sources)[1]
             att_buf[i, cut_of(tiles), side * width : (side + 1) * width] = attended.T.astype(bf16)
 
     chunk = min(4 * TILE, features)
@@ -318,7 +318,7 @@
 
         def body(n, carry):
             cut = pl.ds(pl.multiple_of(n * chunk, chunk), chunk)
-            product = jnp.dot(left, w_buf[i, :, cut], preferred_element_type=f32)
+            product = jnp.dot(left, w_buf[i - 1, :, cut], preferred_element_type=f32)
             if initial:
                 update[:, cut] = state_buf[:, cut].astype(f32) + product
             else:
@@ -338,52 +338,89 @@
         if s > LAG and s % 2 == 0:
             i = s // 2 - 1
             if i == 1:
-                pltpu.make_async_copy(w_buf, w_buf, w_sem).wait()
+                pltpu.make_async_copy(w_buf, w_buf, w_sem.at[0]).wait()
+                pltpu.make_async_copy(w_last, w_last, w_sem.at[1]).wait()
                 state_copy.wait()
                 gain_copy.wait()
             combine(i)
             project(i, i == 1)
 
-    strips = [slice(n, n + 2 * TILE) for n in range(0, features, 2 * TILE)]
-
-    def add_product(i, tiles):
-        cut = cut_of(tiles)
-        left = att_buf[i, cut, :]
-        squares = jnp.zeros((len(tiles) * TILE, TILE), f32)
-        for strip in strips:
-            mixed = update[cut, strip] + jnp.dot(
-                left, w_buf[i, :, strip], preferred_element_type=f32
-            )
-            update[cut, strip] = mixed
-            squares = squares + mixed[:, :TILE] * mixed[:, :TILE]
-            squares = squares + mixed[:, TILE:] * mixed[:, TILE:]
-        return squares
-
     wait_stat(SLOTS - 2)
     for tile in range(blocks):
         wait_tile(SLOTS - 2, tile)
         combine(half - 1, [tile])
-        add_product(half - 1, [tile])
+        cut = cut_of([tile])
+        add_product(att_buf[half - 1, cut, :], w_buf.at[half - 2], update.at[cut], update.at[cut])
+        active = jnp.full(active_ref.shape[1:], halt[tile * TILE] > STEP)
+        active_ref[tile] = active.astype(f32)
 
     wait_stat(SLOTS - 1)
-    for tiles in ([0], list(range(1, blocks))):
-        for tile in tiles:
-            wait_tile(SLOTS - 1, tile)
-        combine(0, tiles)
-        squares = add_product(0, tiles)
-        inverse = lax.rsqrt(jnp.sum(squares, axis=-1, keepdims=True) / features + 1e-06)
-        for strip in strips:
-            gain = gain_buf[strip].astype(f32).reshape(1, -1)
-            for tile in tiles:
-                cut, own_cut = cut_of([tile]), cut_of([tile - tiles[0]])
-                active = jnp.full((TILE, 2 * TILE), halt[tile * TILE] > STEP).astype(bf16) > 0.5
-                normed = (update[cut, strip] * inverse[own_cut] * gain).astype(bf16)
-                out_ref[cut, strip] = jnp.where(active, normed, state_buf[cut, strip])
+    wait_tile(SLOTS - 1, 0)
+    combine(0, [0])
+    cut = cut_of([0])
+    squares = add_product(att_buf[0, cut, :], w_last, update.at[cut], update.at[cut])
+    normalize(squares, update.at[cut], gain_buf, active_ref[0], state_buf.at[cut], first_ref)
+    rest = list(range(1, blocks))
+    for tile in rest:
+        wait_tile(SLOTS - 1, tile)
+    combine(0, rest)
+    left_ref[...] = att_buf[0, cut_of(rest), :]
 
     remote(slot_out, slot_in, slot_send, slot_recv.at[0], 0).wait_send()
     remote(stat_out, stat_in, stat_send, stat_recv.at[0], 0).wait_send()
     for axis in axes:
         remote(flag_out, flag_in.at[axis], flag_send.at[axis], flag_recv, axis).wait_send()
+
+
+def strips_of(ref):
+    return [slice(n, n + 2 * TILE) for n in range(0, ref.shape[1], 2 * TILE)]
+
+
+def add_product(left, weight, base, mixed):
+    squares = jnp.zeros((left.shape[0], TILE), jnp.float32)
+    for strip in strips_of(base):
+        product = jnp.dot(left, weight[:, strip], preferred_element_type=jnp.float32)
+        total = base[:, strip] + product
+        mixed[:, strip] = total
+        squares = squares + total[:, :TILE] * total[:, :TILE]
+        squares = squares + total[:, TILE:] * total[:, TILE:]
+    return squares
+
+
+def normalize(squares, mixed, gain_ref, active, state, out):
+    mean = jnp.sum(squares, axis=-1, keepdims=True) / mixed.shape[1]
+    inverse = lax.rsqrt(mean + 1e-06)
+    chosen = jnp.broadcast_to(active[0:1, :].astype(jnp.bfloat16), (TILE, TILE))
+    chosen = jnp.concatenate([chosen, chosen], axis=1) > 0.5
+    for strip in strips_of(mixed):
+        gain = gain_ref[strip].astype(jnp.float32).reshape(1, -1)
+        normed = (mixed[:, strip] * inverse * gain).astype(jnp.bfloat16)
+        out[:, strip] = jnp.where(chosen, normed, state[:, strip])
+
+
+def finish_kernel(
+    first_ref, left_ref, update, w_last, state_ref, gain_ref, active_ref, out_hbm, mixed, done, sem
+):
+    def store(source, tile):
+        copy = pltpu.make_async_copy(source, out_hbm.at[pl.ds(tile * TILE, TILE)], sem.at[tile])
+        copy.start()
+        return copy
+
+    copies = [store(first_ref, 0)]
+    squares = add_product(left_ref[...], w_last, update.at[pl.ds(TILE, mixed.shape[0])], mixed)
+    for tile in range(mixed.shape[0] // TILE):
+        cut, full = pl.ds(tile * TILE, TILE), pl.ds((tile + 1) * TILE, TILE)
+        normalize(
+            squares[tile * TILE : (tile + 1) * TILE],
+            mixed.at[cut],
+            gain_ref,
+            active_ref[tile + 1],
+            state_ref.at[full],
+            done.at[cut],
+        )
+        copies.append(store(done.at[cut], tile + 1))
+    for copy in copies:
+        copy.wait()
 
 
 def on_star(state_rows, q, k, v, halt_counts, out_weight, norm_gain):
@@ -395,31 +432,37 @@
     vmem = pl.BlockSpec(memory_space=pltpu.VMEM)
     dma = pltpu.SemaphoreType.DMA
     operands = (halt_counts, q, k, v, state_rows, out_weight, norm_gain)
-    return pl.pallas_call(
+    handed = (
+        ((TILE, features), bf16),
+        ((rows - TILE, 2 * width), bf16),
+        ((rows, features), f32),
+        ((2 * width, features), bf16),
+        ((rows, features), bf16),
+        ((features,), bf16),
+        ((blocks, 8, TILE), f32),
+    )
+    results = pl.pallas_call(
         star_kernel,
-        out_shape=jax.ShapeDtypeStruct((rows, features), bf16),
+        out_shape=[jax.ShapeDtypeStruct(*each) for each in handed],
         in_specs=[hbm] * len(operands),
-        out_specs=vmem,
+        out_specs=[vmem] * len(handed),
         scratch_shapes=[
             pltpu.SMEM((rows,), jnp.int32),
-            pltpu.VMEM((features,), bf16),
             pltpu.VMEM((8, width), f32),
             pltpu.VMEM((2, 8, width), f32),
             pltpu.VMEM((3 * heads, rows, width), bf16),
             pltpu.VMEM((SLOTS, 2, blocks, TILE, width), bf16),
             pltpu.VMEM((SLOTS, 2, blocks, TILE, width), bf16),
-            pltpu.VMEM((stats, 2, 2, rows), f32),
-            pltpu.VMEM((stats, 2, 2, rows), f32),
+            pltpu.VMEM((stats, 2, 1, rows), f32),
+            pltpu.VMEM((stats, 2, 1, rows), f32),
             pltpu.VMEM((heads, width, rows), f32),
-            pltpu.VMEM((heads, 2, rows), f32),
+            pltpu.VMEM((heads, 1, rows), f32),
             pltpu.VMEM((half, rows, 2 * width), bf16),
-            pltpu.VMEM((rows, features), bf16),
-            pltpu.VMEM((half, 2 * width, features), bf16),
-            pltpu.VMEM((rows, features), f32),
+            pltpu.VMEM((half - 1, 2 * width, features), bf16),
             dma,
             dma,
             dma,
-            dma,
+            dma((2,)),
             dma((2,)),
             dma,
             dma,
@@ -433,6 +476,18 @@
             collective_id=0, has_side_effects=True, vmem_limit_bytes=32 * 1024 * 1024
         ),
     )(*[pltpu.with_memory_space_constraint(x, pltpu.HBM) for x in operands])
+    return pl.pallas_call(
+        finish_kernel,
+        out_shape=jax.ShapeDtypeStruct((rows, features), bf16),
+        in_specs=[vmem] * len(handed),
+        out_specs=hbm,
+        scratch_shapes=[
+            pltpu.VMEM((rows - TILE, features), f32),
+            pltpu.VMEM((rows - TILE, features), bf16),
+            dma((blocks,)),
+        ],
+        compiler_params=pltpu.CompilerParams(vmem_limit_bytes=8 * 1024 * 1024),
+    )(*results)
 
 
 def fold_heads(carry, queries, key_piece, value_piece, score_scale):

time: 28.9 us -> 28.5 us (0.986)
  local copies, waits for them, and re-layouts: 1.15 us -> 0 us
  Pallas kernels: 27.6 us -> 28.4 us
    unnamed x1 -> x0, local copies, waits for them, and re-layouts: 1.15 us -> none
    pallas_call x1 -> x2, Pallas kernels: 27.6 us -> 28.4 us  [the longest x1 26.7 us: on_star(): pl.pallas_call(star_kernel, out_shape=[jax.ShapeDtypeStruct(*each) for ea...]
where the time goes in v6:
time: 28.5 us; the launch traced here: 28.4 us
  Pallas kernels  28.4 us (100%)
    pallas_call x1, Pallas kernels, on_star(): pl.pallas_call(star_kernel, out_shape=[jax.ShapeDtypeStruct(*each) for ea...  26.7 us
    pallas_call x1, Pallas kernels, on_star(): pl.pallas_call(finish_kernel, out_shape=jax.ShapeDtypeStruct((rows, featu...  1.66 us

profile of v6, /device:TPU:0, one launch (start us, length us, event | category | flops | bytes accessed | tf_op | source)
XLA Modules:
  0.0 28.4 jit_solution(12298372721744574223)
XLA Ops:
  0.0 26.7 %shard_map.73 = (bf16[128,2048]{1,0:T(8,128)(2,1)S(1)}, bf16[256,256]{1,0:T(8,128)(2,1)S(1)}, f32[384,2048]{1,0:T(8,128)S(1)}, bf16[256,2048]{1,0:T(8,128)(2,1)S...) custom-call(s32[384]{0:T(512)} %halt_hbm.1, ...), custom_call_target="tpu_custom_call" | custom-call | tf_op jit(solution)/shard_map/pallas_call | solution.py:444
  26.7 1.7 %shard_map.74 = bf16[384,2048]{1,0:T(8,128)(2,1)} custom-call(bf16[128,2048]{1,0:T(8,128)(2,1)S(1)} %get-tuple-element.12.first_ref, bf16[256,256]{1,0:T(8,128)(2,1)S(1)} %get-tuple-element.13.left_ref, f32[384,2048]{1,0:T(8,128)S(1)} %get-tuple-element.14.update, bf16[256,2048]{1,0:T(8,128)(2,1)S(1)} %get-tuple-element.15.w_last, ...), custom_call_target="tpu_custom_call" | custom-call | tf_op jit(solution)/shard_map/pallas_call | solution.py:479

commit v7 on v6

--- a/solution.py
+++ b/solution.py
@@ -9,17 +9,17 @@
 
 STEP = 2
 TILE = 128
-LAG = 3
-SLOTS = 3 * LAG + 1
+LEAD = 8
 LOG2E = 1.4426950408889634
 
 
-def slot_orders(heads):
+def head_orders(heads):
     half = heads // 2
-    first = [half]
-    singles = [heads - 1, 0]
+    singles = [0, heads - 1, heads - 2]
+    first = []
     for j in range(half - 1):
-        first += [j + 1] + singles[j : j + 1]
+        first += [singles[j], j + 1]
+    first.append(half)
     return first, [(h + half) % heads for h in first]
 
 
@@ -42,8 +42,9 @@
     flag_out,
     flag_in,
     qkv_buf,
-    slot_out,
-    slot_in,
+    tile_out,
+    tile_in,
+    far_part,
     stat_out,
     stat_in,
     own_part,
@@ -56,10 +57,9 @@
     w_sem,
     flag_send,
     flag_recv,
-    slot_send,
+    tile_send,
     stat_send,
     qkv_sem,
-    slot_recv,
     tile_recv,
     stat_recv,
 ):
@@ -69,11 +69,13 @@
     heads, rows, width = q_hbm.shape
     features = state_hbm.shape[1]
     half = heads // 2
-    early = heads - 2
+    steps = heads - 1
+    inputs = heads - 2
     blocks = rows // TILE
+    meeting = blocks
     scale = width ** (-0.5) * LOG2E
     axes = (0, 1)
-    orders = slot_orders(heads)
+    orders = head_orders(heads)
     f32, bf16 = jnp.float32, jnp.bfloat16
 
     def local(src, dst, sem):
@@ -98,14 +100,14 @@
         )
     halt_copy = local(halt_hbm, halt, halt_sem)
 
-    def choices(s, axis):
-        return (0, orders[axis][s]), (1 + s % 2, orders[1 - axis][2 * (s // 2) + 1])
+    def choices(b, axis):
+        return (0, orders[axis][b]), (1 + b % 2, orders[1 - axis][2 * (b // 2) + 1])
 
     group_of = {}
-    for s in range(LAG):
+    for b in range(blocks):
         for axis in axes:
-            for block in choices(s, axis):
-                group_of[block] = min(s, 1)
+            for block in choices(b, axis):
+                group_of[block] = min(b, 1)
     for block in [(n, h) for h in range(heads) for n in range(3)]:
         group_of.setdefault(block, 2)
     for (n, h), group in group_of.items():
@@ -129,45 +131,58 @@
 
     is_owner = mask(flag)
 
-    def opening(s, axis):
-        mine, other = choices(s, axis)
-        return jnp.where(is_owner, own(*mine), own(*other))
-
-    def send(s):
-        if s < SLOTS - 2:
-            for axis in axes:
-                remote(
-                    slot_out.at[s, axis], slot_in.at[s, axis], slot_send, slot_recv.at[s], axis
-                ).start()
-            return
-        for tile in range(blocks):
-            for axis in axes:
-                remote(
-                    slot_out.at[s, axis, tile],
-                    slot_in.at[s, axis, tile],
-                    slot_send,
-                    tile_recv.at[s - SLOTS + 2, tile],
-                    axis,
-                ).start()
-
-    def wait_tile(s, tile):
-        landed = slot_in.at[s, pl.ds(0, 2), tile]
-        remote(landed, landed, slot_send, tile_recv.at[s - SLOTS + 2, tile], 0).wait_recv()
-
-    def wait_stat(s):
-        stat = s - LAG - 1
-        remote(
-            stat_in.at[stat], stat_in.at[stat], stat_send, stat_recv.at[stat], 0
-        ).wait_recv()
-
-    for s in range(LAG):
+    def cut_of(tiles):
+        return slice(tiles[0] * TILE, (tiles[-1] + 1) * TILE)
+
+    def input_tile(u, axis):
+        b, cut = u // blocks, cut_of([u % blocks])
+        if b < inputs:
+            mine, other = choices(b, axis)
+            return jnp.where(is_owner[cut], own(*mine)[cut], own(*other)[cut])
+        return jnp.where(is_owner[cut], own(0, orders[axis][b])[cut], far_part[axis, :, cut])
+
+    groups = [(u, min(blocks, LEAD - u)) for u in range(0, LEAD, blocks)]
+    for p in range(steps):
+        groups += [(LEAD + blocks * p, 1), (LEAD + blocks * p + 1, blocks - 1)]
+
+    def send(n):
+        start, count = groups[n]
         for axis in axes:
-            slot_out[s, axis] = opening(s, axis).reshape(blocks, TILE, width)
-        if s == 0:
+            remote(
+                tile_out.at[axis, pl.ds(start, count)],
+                tile_in.at[axis, pl.ds(start, count)],
+                tile_send,
+                tile_recv.at[n],
+                axis,
+            ).start()
+
+    waited = []
+
+    def wait_tiles(u):
+        while sum(count for _, count in groups[: len(waited)]) <= u:
+            n = len(waited)
+            start, count = groups[n]
+            landed = tile_in.at[pl.ds(0, 2), pl.ds(start, count)]
+            remote(landed, landed, tile_send, tile_recv.at[n], 0).wait_recv()
+            waited.append(n)
+
+    known = []
+
+    def wait_stats(p):
+        while len(known) <= p:
+            n = len(known)
+            remote(stat_in.at[n], stat_in.at[n], stat_send, stat_recv.at[n], 0).wait_recv()
+            known.append(n)
+
+    for n, (start, count) in enumerate(groups[: len(range(0, LEAD, blocks))]):
+        for axis in axes:
+            for u in range(start, start + count):
+                tile_out[axis, u] = input_tile(u, axis)
+        if n == 0:
             pl.semaphore_wait(barrier, 2)
             for axis in axes:
                 remote(flag_out, flag_in.at[axis], flag_send.at[axis], flag_recv, axis).start()
-        send(s)
+        send(n)
 
     for side in (0, 1):
         cut = pl.ds(side * width, width)
@@ -184,8 +199,8 @@
     def bias(valid):
         return jnp.concatenate([(valid[0:1, :] - 1.0) * 1e30] * blocks, axis=1)
 
-    def received(s, axis):
-        return slot_in[s, axis].reshape(rows, width)
+    def received(b, axis):
+        return tile_in[axis, b * blocks : (b + 1) * blocks].reshape(rows, width)
 
     def attend(query, keys, values):
         scores = lax.dot_general(
@@ -207,40 +222,36 @@
         parts = [part * (each * inverse) for each, (_, part) in zip(sums, sources)]
         return top + jnp.log2(total), functools.reduce(jnp.add, parts)
 
-    def put(s, results):
+    def put(p, level, part, query=None):
+        part = part.astype(bf16)
         for axis in axes:
-            stat_out[s - LAG - 1, axis], part = results[axis]
-            part = part.astype(bf16)
-            block = opening(s, axis) if s < early else None
+            stat_out[p, axis] = level[axis]
             for tile in range(blocks):
-                cut = slice(tile * TILE, (tile + 1) * TILE)
+                u, cut = LEAD + blocks * p + tile, cut_of([tile])
                 piece = part[:, cut]
-                if s < early:
-                    piece = jnp.where(is_beside[cut], piece, block[cut])
-                slot_out[s, axis, tile] = piece
+                if query is not None:
+                    piece = jnp.where(owner_at[1 - axis][cut], query[cut], piece)
+                if u < steps * blocks:
+                    piece = jnp.where(is_beside[cut], piece, input_tile(u, axis))
+                tile_out[axis, u] = piece
             remote(
-                stat_out.at[s - LAG - 1, axis],
-                stat_in.at[s - LAG - 1, axis],
-                stat_send,
-                stat_recv.at[s - LAG - 1],
-                axis,
+                stat_out.at[p, axis], stat_in.at[p, axis], stat_send, stat_recv.at[p], axis
             ).start()
-        send(s)
+        first = len(groups) - 2 * (steps - p)
+        send(first)
+        send(first + 1)
 
     def keep(h, result):
         own_stat[h], own_part[h] = result
-
-    def cut_of(tiles):
-        return slice(tiles[0] * TILE, (tiles[-1] + 1) * TILE)
 
     def kept(h, tiles=range(blocks)):
         cut = cut_of(tiles)
         return own_stat[h, :, cut], own_part[h, :, cut]
 
-    def sent(s, axis, tiles=range(blocks)):
-        cut, stat = cut_of(tiles), s - LAG - 1
-        block = jnp.concatenate([slot_in[s, axis, tile] for tile in tiles], axis=1)
-        return stat_in[stat, axis, :, cut], block.astype(f32)
+    def sent(p, axis, tiles=range(blocks), start=None):
+        start = LEAD + blocks * p if start is None else start
+        block = jnp.concatenate([tile_in[axis, start + tile] for tile in tiles], axis=1)
+        return stat_in[p, axis, :, cut_of(tiles)], block.astype(f32)
 
     def select(value, first, second):
         line = jnp.concatenate([value[0:1, :]] * blocks, axis=1)
@@ -258,47 +269,44 @@
         if s % 2 == 0:
             result = attend(query, key, value)
             keep(low, result)
-            if s > 0:
-                put(s + LAG, (result, result))
-            else:
-                for axis in axes:
-                    block = jnp.where(owner_at[1 - axis], query, opening(LAG, axis))
-                    slot_out[LAG, axis] = block.reshape(blocks, TILE, width)
-                send(LAG)
+            if s == inputs:
+                start, p = s * blocks, meeting
+                far = select(
+                    flag_in[0], sent(p, 1, start=start), sent(p, 0, start=start)
+                )
+                result = merge((result, far))
+            put(s, [result[0]] * 2, result[1], query if s == 0 else None)
             return
         far_key = jnp.where(owner_at[0], received(s - 1, 1), received(s - 1, 0))
         far_value = jnp.where(owner_at[0], received(s, 1), received(s, 0))
         far_query = query
-        valid = beside if s > LAG else beside + flag
-        if s == LAG:
-            far, near = orders[0][0], orders[1][0]
+        valid = beside + flag if s == 1 else beside
+        if s == meeting:
+            one, two = (
+                jnp.concatenate([tile_in[axis, LEAD + tile] for tile in range(blocks)], axis=0)
+                for axis in axes
+            )
             take = mask(flag + beside)
-            query = jnp.where(take, query, received(s, 1))
-            key = jnp.where(take, key, own(1, far))
-            value = jnp.where(take, value, own(2, far))
-            far_query = jnp.where(take, far_query, received(s, 0))
-            far_key = jnp.where(take, far_key, own(1, near))
-            far_value = jnp.where(take, far_value, own(2, near))
+            query = jnp.where(take, query, two)
+            key = jnp.where(take, key, own(1, orders[0][0]))
+            value = jnp.where(take, value, own(2, orders[0][0]))
+            far_query = jnp.where(take, far_query, one)
+            far_key = jnp.where(take, far_key, own(1, orders[1][0]))
+            far_value = jnp.where(take, far_value, own(2, orders[1][0]))
         nearby = attend(query, key, value)
         distant = attend(far_query, far_key, far_value)
         result = merge((nearby, (distant[0] + bias(valid), distant[1])))
         keep(low, result)
-        if s == LAG:
-            put(
-                s + LAG,
-                (select(beside, result, distant), select(beside, result, nearby)),
-            )
-        else:
-            put(s + LAG, (result, result))
-        if s <= LAG:
+        level = [result[0]] * 2
+        if s == meeting:
+            for axis, each in enumerate((nearby, distant)):
+                far_part[axis] = each[1].astype(bf16)
+                level[axis] = select(beside, result[:1], each[:1])[0]
+        put(s, level, result[1])
+        if s == 1:
             nearby = attend(own(0, high), own(1, high), own(2, high))
             distant = attend(own(0, high), received(s - 1, 1), received(s, 1))
             keep(high, merge((nearby, distant)))
-
-    def finish_first():
-        near, far = orders[1][0], 2 * LAG
-        result = merge((kept(near), select(flag_in[0], sent(far, 1), sent(far, 0))))
-        put(SLOTS - 1, (result, result))
 
     def combine(i, tiles=range(blocks)):
         for side in (0, 1):
@@ -306,8 +314,7 @@
             sources = [kept(h, tiles)]
             for axis in axes:
                 if h in orders[axis]:
-                    s = orders[axis].index(h)
-                    sources.append(sent(s + LAG if s > 0 else SLOTS - 1, axis, tiles))
+                    sources.append(sent(orders[axis].index(h), axis, tiles))
             attended = merge(sources)[1]
             att_buf[i, cut_of(tiles), side * width : (side + 1) * width] = attended.T.astype(bf16)
 
@@ -327,53 +334,59 @@
 
         lax.fori_loop(0, features // chunk, body, 0)
 
-    for s in range(SLOTS - 2):
-        remote(slot_in.at[s], slot_in.at[s], slot_send, slot_recv.at[s], 0).wait_recv()
-        if s > LAG:
-            wait_stat(s)
-        if s < early:
-            step(s)
-        elif s == early:
-            finish_first()
-        if s > LAG and s % 2 == 0:
-            i = s // 2 - 1
-            if i == 1:
-                pltpu.make_async_copy(w_buf, w_buf, w_sem.at[0]).wait()
-                pltpu.make_async_copy(w_last, w_last, w_sem.at[1]).wait()
-                state_copy.wait()
-                gain_copy.wait()
-            combine(i)
-            project(i, i == 1)
-
-    wait_stat(SLOTS - 2)
-    for tile in range(blocks):
-        wait_tile(SLOTS - 2, tile)
-        combine(half - 1, [tile])
-        cut = cut_of([tile])
-        add_product(att_buf[half - 1, cut, :], w_buf.at[half - 2], update.at[cut], update.at[cut])
-        active = jnp.full(active_ref.shape[1:], halt[tile * TILE] > STEP)
-        active_ref[tile] = active.astype(f32)
-
-    wait_stat(SLOTS - 1)
-    wait_tile(SLOTS - 1, 0)
+    def result_tile(p, tile):
+        return LEAD + blocks * p + tile
+
+    for s in range(steps):
+        wait_tiles((s + 1) * blocks - 1)
+        if s == inputs:
+            wait_stats(meeting)
+        step(s)
+        if s == half:
+            pltpu.make_async_copy(w_buf, w_buf, w_sem.at[0]).wait()
+            pltpu.make_async_copy(w_last, w_last, w_sem.at[1]).wait()
+            state_copy.wait()
+            gain_copy.wait()
+            wait_stats(1)
+            combine(1)
+            project(1, True)
+    for i in range(2, half - 1):
+        p = max(order.index(i) for order in orders)
+        wait_tiles(result_tile(p, blocks - 1))
+        wait_stats(p)
+        combine(i)
+        project(i, False)
+
+    i, p, rest = half - 1, steps - 2, list(range(1, blocks))
+    for tiles in ([0], rest):
+        wait_tiles(result_tile(p, tiles[-1]))
+        wait_stats(p)
+        combine(i, tiles)
+        cut = cut_of(tiles)
+        add_product(att_buf[i, cut, :], w_buf.at[i - 1], update.at[cut], update.at[cut])
+        for tile in tiles:
+            active = jnp.full(active_ref.shape[1:], halt[tile * TILE] > STEP)
+            active_ref[tile] = active.astype(f32)
+
+    p = steps - 1
+    wait_stats(p)
+    wait_tiles(result_tile(p, 0))
     combine(0, [0])
     cut = cut_of([0])
     squares = add_product(att_buf[0, cut, :], w_last, update.at[cut], update.at[cut])
     normalize(squares, update.at[cut], gain_buf, active_ref[0], state_buf.at[cut], first_ref)
-    rest = list(range(1, blocks))
-    for tile in rest:
-        wait_tile(SLOTS - 1, tile)
+    wait_tiles(result_tile(p, blocks - 1))
     combine(0, rest)
     left_ref[...] = att_buf[0, cut_of(rest), :]
 
-    remote(slot_out, slot_in, slot_send, slot_recv.at[0], 0).wait_send()
+    remote(tile_out, tile_in, tile_send, tile_recv.at[0], 0).wait_send()
     remote(stat_out, stat_in, stat_send, stat_recv.at[0], 0).wait_send()
     for axis in axes:
         remote(flag_out, flag_in.at[axis], flag_send.at[axis], flag_recv, axis).wait_send()
 
 
 def strips_of(ref):
-    return [slice(n, n + 2 * TILE) for n in range(0, ref.shape[1], 2 * TILE)]
+    return [slice(n, n + 4 * TILE) for n in range(0, ref.shape[1], 4 * TILE)]
 
 
 def add_product(left, weight, base, mixed):
@@ -382,8 +395,8 @@
         product = jnp.dot(left, weight[:, strip], preferred_element_type=jnp.float32)
         total = base[:, strip] + product
         mixed[:, strip] = total
-        squares = squares + total[:, :TILE] * total[:, :TILE]
-        squares = squares + total[:, TILE:] * total[:, TILE:]
+        for n in range(0, total.shape[1], TILE):
+            squares = squares + total[:, n : n + TILE] * total[:, n : n + TILE]
     return squares
 
 
@@ -391,7 +404,7 @@
     mean = jnp.sum(squares, axis=-1, keepdims=True) / mixed.shape[1]
     inverse = lax.rsqrt(mean + 1e-06)
     chosen = jnp.broadcast_to(active[0:1, :].astype(jnp.bfloat16), (TILE, TILE))
-    chosen = jnp.concatenate([chosen, chosen], axis=1) > 0.5
+    chosen = jnp.concatenate([chosen] * 4, axis=1) > 0.5
     for strip in strips_of(mixed):
         gain = gain_ref[strip].astype(jnp.float32).reshape(1, -1)
         normed = (mixed[:, strip] * inverse * gain).astype(jnp.bfloat16)
@@ -426,7 +439,9 @@
 def on_star(state_rows, q, k, v, halt_counts, out_weight, norm_gain):
     heads, rows, width = q.shape
     features = state_rows.shape[1]
-    half, blocks, stats = heads // 2, rows // TILE, SLOTS - LAG - 1
+    half, blocks, steps = heads // 2, rows // TILE, heads - 1
+    tiles = LEAD + steps * blocks
+    groups = pl.cdiv(LEAD, blocks) + 2 * steps
     bf16, f32 = jnp.bfloat16, jnp.float32
     hbm = pl.BlockSpec(memory_space=pltpu.MemorySpace.HBM)
     vmem = pl.BlockSpec(memory_space=pltpu.VMEM)
@@ -451,10 +466,11 @@
             pltpu.VMEM((8, width), f32),
             pltpu.VMEM((2, 8, width), f32),
             pltpu.VMEM((3 * heads, rows, width), bf16),
-            pltpu.VMEM((SLOTS, 2, blocks, TILE, width), bf16),
-            pltpu.VMEM((SLOTS, 2, blocks, TILE, width), bf16),
-            pltpu.VMEM((stats, 2, 1, rows), f32),
-            pltpu.VMEM((stats, 2, 1, rows), f32),
+            pltpu.VMEM((2, tiles, TILE, width), bf16),
+            pltpu.VMEM((2, tiles, TILE, width), bf16),
+            pltpu.VMEM((2, width, rows), bf16),
+            pltpu.VMEM((steps, 2, 1, rows), f32),
+            pltpu.VMEM((steps, 2, 1, rows), f32),
             pltpu.VMEM((heads, width, rows), f32),
             pltpu.VMEM((heads, 1, rows), f32),
             pltpu.VMEM((half, rows, 2 * width), bf16),
@@ -468,9 +484,8 @@
             dma,
             dma,
             dma((3,)),
-            dma((SLOTS - 2,)),
-            dma((2, blocks)),
-            dma((stats,)),
+            dma((groups,)),
+            dma((steps,)),
         ],
         compiler_params=pltpu.CompilerParams(
             collective_id=0, has_side_effects=True, vmem_limit_bytes=32 * 1024 * 1024
@@ -557,7 +572,7 @@
     def per_device(state_rows, q, k, v, halt_counts, out_weight, norm_gain):
         heads, rows, width = q.shape
         one_owner = rows == (n_ctx - 1) * TILE
-        if one_owner and heads - 2 == 2 * LAG and width == TILE and n_ctx == 4:
+        if one_owner and heads == LEAD and width == TILE and n_ctx == 4:
             return on_star(state_rows, q, k, v, halt_counts, out_weight, norm_gain)
         return on_device(state_rows, q, k, v, halt_counts, out_weight, norm_gain)
 

time: 28.5 us -> 27.9 us (0.979)
  Pallas kernels: 28.4 us -> 27.8 us
    pallas_call x1, Pallas kernels: 26.7 us -> 26.1 us  [on_star(): pl.pallas_call(star_kernel, out_shape=[jax.ShapeDtypeStruct(*each) for ea...]
where the time goes in v7:
time: 27.9 us; the launch traced here: 27.8 us
  Pallas kernels  27.8 us (100%)
    pallas_call x1, Pallas kernels, on_star(): pl.pallas_call(star_kernel, out_shape=[jax.ShapeDtypeStruct(*each) for ea...  26.1 us
    pallas_call x1, Pallas kernels, on_star(): pl.pallas_call(finish_kernel, out_shape=jax.ShapeDtypeStruct((rows, featu...  1.66 us

profile of v7, /device:TPU:0, one launch (start us, length us, event | category | flops | bytes accessed | tf_op | source)
XLA Modules:
  0.0 27.8 jit_solution(7312535556149793714)
XLA Ops:
  0.0 26.1 %shard_map.73 = (bf16[128,2048]{1,0:T(8,128)(2,1)S(1)}, bf16[256,256]{1,0:T(8,128)(2,1)S(1)}, f32[384,2048]{1,0:T(8,128)S(1)}, bf16[256,2048]{1,0:T(8,128)(2,1)S...) custom-call(s32[384]{0:T(512)} %halt_hbm.1, ...), custom_call_target="tpu_custom_call" | custom-call | tf_op jit(solution)/shard_map/pallas_call | solution.py:459
  26.1 1.7 %shard_map.74 = bf16[384,2048]{1,0:T(8,128)(2,1)} custom-call(bf16[128,2048]{1,0:T(8,128)(2,1)S(1)} %get-tuple-element.12.first_ref, bf16[256,256]{1,0:T(8,128)(2,1)S(1)} %get-tuple-element.13.left_ref, f32[384,2048]{1,0:T(8,128)S(1)} %get-tuple-element.14.update, bf16[256,2048]{1,0:T(8,128)(2,1)S(1)} %get-tuple-element.15.w_last, ...), custom_call_target="tpu_custom_call" | custom-call | tf_op jit(solution)/shard_map/pallas_call | solution.py:494

commit v8 on v7

--- a/solution.py
+++ b/solution.py
@@ -419,21 +419,35 @@
         copy.start()
         return copy
 
-    copies = [store(first_ref, 0)]
-    squares = add_product(left_ref[...], w_last, update.at[pl.ds(TILE, mixed.shape[0])], mixed)
-    for tile in range(mixed.shape[0] // TILE):
-        cut, full = pl.ds(tile * TILE, TILE), pl.ds((tile + 1) * TILE, TILE)
-        normalize(
-            squares[tile * TILE : (tile + 1) * TILE],
-            mixed.at[cut],
-            gain_ref,
-            active_ref[tile + 1],
-            state_ref.at[full],
-            done.at[cut],
-        )
-        copies.append(store(done.at[cut], tile + 1))
-    for copy in copies:
-        copy.wait()
+    tiles = range(1, 1 + mixed.shape[0] // TILE)
+    first = store(first_ref, 0)
+    some_active = jnp.max(active_ref[pl.ds(1, len(tiles))]) > 0.5
+
+    @pl.when(some_active)
+    def _():
+        squares = add_product(left_ref[...], w_last, update.at[pl.ds(TILE, mixed.shape[0])], mixed)
+        copies = []
+        for tile in tiles:
+            cut = pl.ds((tile - 1) * TILE, TILE)
+            normalize(
+                squares[(tile - 1) * TILE : tile * TILE],
+                mixed.at[cut],
+                gain_ref,
+                active_ref[tile],
+                state_ref.at[pl.ds(tile * TILE, TILE)],
+                done.at[cut],
+            )
+            copies.append(store(done.at[cut], tile))
+        for copy in copies:
+            copy.wait()
+
+    @pl.when(jnp.logical_not(some_active))
+    def _():
+        copies = [store(state_ref.at[pl.ds(tile * TILE, TILE)], tile) for tile in tiles]
+        for copy in copies:
+            copy.wait()
+
+    first.wait()
 
 
 def on_star(state_rows, q, k, v, halt_counts, out_weight, norm_gain):

time: 27.9 us -> 27.4 us (0.982)
  Pallas kernels: 27.8 us -> 27.3 us
    pallas_call x1, Pallas kernels: 1.66 us -> 1.17 us  [on_star(): pl.pallas_call(finish_kernel, out_shape=jax.ShapeDtypeStruct((rows, featu...]
where the time goes in v8:
time: 27.4 us; the launch traced here: 27.3 us
  Pallas kernels  27.3 us (100%)
    pallas_call x1, Pallas kernels, on_star(): pl.pallas_call(star_kernel, out_shape=[jax.ShapeDtypeStruct(*each) for ea...  26.1 us
    pallas_call x1, Pallas kernels, on_star(): pl.pallas_call(finish_kernel, out_shape=jax.ShapeDtypeStruct((rows, featu...  1.17 us

profile of v8, /device:TPU:0, one launch (start us, length us, event | category | flops | bytes accessed | tf_op | source)
XLA Modules:
  0.0 27.3 jit_solution(12584548741974295241)
XLA Ops:
  0.0 26.1 %shard_map.73 = (bf16[128,2048]{1,0:T(8,128)(2,1)S(1)}, bf16[256,256]{1,0:T(8,128)(2,1)S(1)}, f32[384,2048]{1,0:T(8,128)S(1)}, bf16[256,2048]{1,0:T(8,128)(2,1)S...) custom-call(s32[384]{0:T(512)} %halt_hbm.1, ...), custom_call_target="tpu_custom_call" | custom-call | tf_op jit(solution)/shard_map/pallas_call | solution.py:473
  26.1 1.2 %shard_map.74 = bf16[384,2048]{1,0:T(8,128)(2,1)} custom-call(bf16[128,2048]{1,0:T(8,128)(2,1)S(1)} %get-tuple-element.12.first_ref, bf16[256,256]{1,0:T(8,128)(2,1)S(1)} %get-tuple-element.13.left_ref, f32[384,2048]{1,0:T(8,128)S(1)} %get-tuple-element.14.update, bf16[256,2048]{1,0:T(8,128)(2,1)S(1)} %get-tuple-element.15.w_last, ...), custom_call_target="tpu_custom_call" | custom-call | tf_op jit(solution)/shard_map/pallas_call | solution.py:508

commit v9 on v8

--- a/solution.py
+++ b/solution.py
@@ -10,6 +10,7 @@
 STEP = 2
 TILE = 128
 LEAD = 8
+STATS = 4
 LOG2E = 1.4426950408889634
 
 
@@ -21,6 +22,21 @@
         first += [singles[j], j + 1]
     first.append(half)
     return first, [(h + half) % heads for h in first]
+
+
+def tile_groups(steps, blocks):
+    groups = [(u, min(blocks, LEAD - u)) for u in range(0, LEAD, blocks)]
+    opening = len(groups)
+    for p in range(steps):
+        groups += [(LEAD + blocks * p, 1), (LEAD + blocks * p + 1, blocks - 1)]
+    sems, last = [], {}
+    for n in range(len(groups)):
+        done = blocks * ((n - opening) // 2 - 1) - 1 if n >= opening else -1
+        free = [sem for sem, end in last.items() if end <= done]
+        sem = free[0] if free else len(last)
+        sems.append(sem)
+        last[sem] = sum(groups[n]) - 1
+    return groups, sems
 
 
 def star_kernel(
@@ -141,9 +157,7 @@
             return jnp.where(is_owner[cut], own(*mine)[cut], own(*other)[cut])
         return jnp.where(is_owner[cut], own(0, orders[axis][b])[cut], far_part[axis, :, cut])
 
-    groups = [(u, min(blocks, LEAD - u)) for u in range(0, LEAD, blocks)]
-    for p in range(steps):
-        groups += [(LEAD + blocks * p, 1), (LEAD + blocks * p + 1, blocks - 1)]
+    groups, group_sems = tile_groups(steps, blocks)
 
     def send(n):
         start, count = groups[n]
@@ -152,7 +166,7 @@
                 tile_out.at[axis, pl.ds(start, count)],
                 tile_in.at[axis, pl.ds(start, count)],
                 tile_send,
-                tile_recv.at[n],
+                tile_recv.at[group_sems[n]],
                 axis,
             ).start()
 
@@ -163,7 +177,7 @@
             n = len(waited)
             start, count = groups[n]
             landed = tile_in.at[pl.ds(0, 2), pl.ds(start, count)]
-            remote(landed, landed, tile_send, tile_recv.at[n], 0).wait_recv()
+            remote(landed, landed, tile_send, tile_recv.at[group_sems[n]], 0).wait_recv()
             waited.append(n)
 
     known = []
@@ -171,7 +185,9 @@
     def wait_stats(p):
         while len(known) <= p:
             n = len(known)
-            remote(stat_in.at[n], stat_in.at[n], stat_send, stat_recv.at[n], 0).wait_recv()
+            remote(
+                stat_in.at[n], stat_in.at[n], stat_send, stat_recv.at[n % STATS], 0
+            ).wait_recv()
             known.append(n)
 
     for n, (start, count) in enumerate(groups[: len(range(0, LEAD, blocks))]):
@@ -181,7 +197,7 @@
         if n == 0:
             pl.semaphore_wait(barrier, 2)
             for axis in axes:
-                remote(flag_out, flag_in.at[axis], flag_send.at[axis], flag_recv, axis).start()
+                remote(flag_out, flag_in.at[axis], flag_send, flag_recv, axis).start()
         send(n)
 
     for side in (0, 1):
@@ -191,7 +207,7 @@
     state_copy = local(state_hbm, state_buf, state_sem)
     gain_copy = local(gain_hbm, gain_buf, gain_sem)
 
-    remote(flag_in, flag_in, flag_send.at[0], flag_recv, 0).wait_recv()
+    remote(flag_in, flag_in, flag_send, flag_recv, 0).wait_recv()
     owner_at = [mask(flag_in[axis]) for axis in axes]
     beside = flag_in[0] + flag_in[1]
     is_beside = mask(beside)
@@ -235,7 +251,11 @@
                     piece = jnp.where(is_beside[cut], piece, input_tile(u, axis))
                 tile_out[axis, u] = piece
             remote(
-                stat_out.at[p, axis], stat_in.at[p, axis], stat_send, stat_recv.at[p], axis
+                stat_out.at[p, axis],
+                stat_in.at[p, axis],
+                stat_send,
+                stat_recv.at[p % STATS],
+                axis,
             ).start()
         first = len(groups) - 2 * (steps - p)
         send(first)
@@ -339,8 +359,7 @@
 
     for s in range(steps):
         wait_tiles((s + 1) * blocks - 1)
-        if s == inputs:
-            wait_stats(meeting)
+        wait_stats(meeting if s == inputs else s - 2)
         step(s)
         if s == half:
             pltpu.make_async_copy(w_buf, w_buf, w_sem.at[0]).wait()
@@ -381,8 +400,7 @@
 
     remote(tile_out, tile_in, tile_send, tile_recv.at[0], 0).wait_send()
     remote(stat_out, stat_in, stat_send, stat_recv.at[0], 0).wait_send()
-    for axis in axes:
-        remote(flag_out, flag_in.at[axis], flag_send.at[axis], flag_recv, axis).wait_send()
+    remote(flag_in, flag_in, flag_send, flag_recv, 0).wait_send()
 
 
 def strips_of(ref):
@@ -455,7 +473,7 @@
     features = state_rows.shape[1]
     half, blocks, steps = heads // 2, rows // TILE, heads - 1
     tiles = LEAD + steps * blocks
-    groups = pl.cdiv(LEAD, blocks) + 2 * steps
+    landings = 1 + max(tile_groups(steps, blocks)[1])
     bf16, f32 = jnp.bfloat16, jnp.float32
     hbm = pl.BlockSpec(memory_space=pltpu.MemorySpace.HBM)
     vmem = pl.BlockSpec(memory_space=pltpu.VMEM)
@@ -493,13 +511,13 @@
             dma,
             dma,
             dma((2,)),
-            dma((2,)),
+            dma,
             dma,
             dma,
             dma,
             dma((3,)),
-            dma((groups,)),
-            dma((steps,)),
+            dma((landings,)),
+            dma((STATS,)),
         ],
         compiler_params=pltpu.CompilerParams(
             collective_id=0, has_side_effects=True, vmem_limit_bytes=32 * 1024 * 1024

time: 27.4 us -> 27.3 us (level)
  no operation moved by 1% of the time
where the time goes in v9:
time: 27.3 us; the launch traced here: 27.2 us
  Pallas kernels  27.2 us (100%)
    pallas_call x1, Pallas kernels, on_star(): pl.pallas_call(star_kernel, out_shape=[jax.ShapeDtypeStruct(*each) for ea...  26 us
    pallas_call x1, Pallas kernels, on_star(): pl.pallas_call(finish_kernel, out_shape=jax.ShapeDtypeStruct((rows, featu...  1.17 us

profile of v9, /device:TPU:0, one launch (start us, length us, event | category | flops | bytes accessed | tf_op | source)
XLA Modules:
  0.0 27.2 jit_solution(14680348473667272840)
XLA Ops:
  0.0 26.0 %shard_map.73 = (bf16[128,2048]{1,0:T(8,128)(2,1)S(1)}, bf16[256,256]{1,0:T(8,128)(2,1)S(1)}, f32[384,2048]{1,0:T(8,128)S(1)}, bf16[256,2048]{1,0:T(8,128)(2,1)S...) custom-call(s32[384]{0:T(512)} %halt_hbm.1, ...), custom_call_target="tpu_custom_call" | custom-call | tf_op jit(solution)/shard_map/pallas_call | solution.py:491
  26.0 1.2 %shard_map.74 = bf16[384,2048]{1,0:T(8,128)(2,1)} custom-call(bf16[128,2048]{1,0:T(8,128)(2,1)S(1)} %get-tuple-element.12.first_ref, bf16[256,256]{1,0:T(8,128)(2,1)S(1)} %get-tuple-element.13.left_ref, f32[384,2048]{1,0:T(8,128)S(1)} %get-tuple-element.14.update, bf16[256,2048]{1,0:T(8,128)(2,1)S(1)} %get-tuple-element.15.w_last, ...), custom_call_target="tpu_custom_call" | custom-call | tf_op jit(solution)/shard_map/pallas_call | solution.py:526

commit v10 on v9

--- a/solution.py
+++ b/solution.py
@@ -68,8 +68,6 @@
     att_buf,
     w_buf,
     halt_sem,
-    gain_sem,
-    state_sem,
     w_sem,
     flag_send,
     flag_recv,
@@ -202,10 +200,10 @@
 
     for side in (0, 1):
         cut = pl.ds(side * width, width)
-        local(w_hbm.at[pl.ds(side * half + 1, half - 1)], w_buf.at[:, cut], w_sem.at[0])
-        local(w_hbm.at[side * half], w_last.at[cut], w_sem.at[1])
-    state_copy = local(state_hbm, state_buf, state_sem)
-    gain_copy = local(gain_hbm, gain_buf, gain_sem)
+        local(w_hbm.at[pl.ds(side * half + 1, half - 1)], w_buf.at[:, cut], qkv_sem.at[1])
+        local(w_hbm.at[side * half], w_last.at[cut], w_sem)
+    state_copy = local(state_hbm, state_buf, qkv_sem.at[0])
+    gain_copy = local(gain_hbm, gain_buf, halt_sem)
 
     remote(flag_in, flag_in, flag_send, flag_recv, 0).wait_recv()
     owner_at = [mask(flag_in[axis]) for axis in axes]
@@ -362,8 +360,8 @@
         wait_stats(meeting if s == inputs else s - 2)
         step(s)
         if s == half:
-            pltpu.make_async_copy(w_buf, w_buf, w_sem.at[0]).wait()
-            pltpu.make_async_copy(w_last, w_last, w_sem.at[1]).wait()
+            pltpu.make_async_copy(w_buf, w_buf, qkv_sem.at[1]).wait()
+            pltpu.make_async_copy(w_last, w_last, w_sem).wait()
             state_copy.wait()
             gain_copy.wait()
             wait_stats(1)
@@ -510,8 +508,6 @@
             dma,
             dma,
             dma,
-            dma((2,)),
-            dma,
             dma,
             dma,
             dma,

time: 27.3 us -> 27.6 us (1.011); the launches traced: 27.2 us -> 27.2 us
  no operation moved by 1% of the time
where the time goes in v10:
time: 27.6 us; the launch traced here: 27.2 us
  Pallas kernels  27.2 us (99%)
    pallas_call x1, Pallas kernels, on_star(): pl.pallas_call(star_kernel, out_shape=[jax.ShapeDtypeStruct(*each) for ea...  26 us
    pallas_call x1, Pallas kernels, on_star(): pl.pallas_call(finish_kernel, out_shape=jax.ShapeDtypeStruct((rows, featu...  1.17 us

profile of v10, /device:TPU:0, one launch (start us, length us, event | category | flops | bytes accessed | tf_op | source)
XLA Modules:
  0.0 27.2 jit_solution(1607439445232448094)
XLA Ops:
  0.0 26.0 %shard_map.73 = (bf16[128,2048]{1,0:T(8,128)(2,1)S(1)}, bf16[256,256]{1,0:T(8,128)(2,1)S(1)}, f32[384,2048]{1,0:T(8,128)S(1)}, bf16[256,2048]{1,0:T(8,128)(2,1)S...) custom-call(s32[384]{0:T(512)} %halt_hbm.1, ...), custom_call_target="tpu_custom_call" | custom-call | tf_op jit(solution)/shard_map/pallas_call | solution.py:489
  26.0 1.2 %shard_map.74 = bf16[384,2048]{1,0:T(8,128)(2,1)} custom-call(bf16[128,2048]{1,0:T(8,128)(2,1)S(1)} %get-tuple-element.12.first_ref, bf16[256,256]{1,0:T(8,128)(2,1)S(1)} %get-tuple-element.13.left_ref, f32[384,2048]{1,0:T(8,128)S(1)} %get-tuple-element.14.update, bf16[256,2048]{1,0:T(8,128)(2,1)S(1)} %get-tuple-element.15.w_last, ...), custom_call_target="tpu_custom_call" | custom-call | tf_op jit(solution)/shard_map/pallas_call | solution.py:522

commit v11 on v10

--- a/solution.py
+++ b/solution.py
@@ -493,8 +493,8 @@
         out_specs=[vmem] * len(handed),
         scratch_shapes=[
             pltpu.SMEM((rows,), jnp.int32),
-            pltpu.VMEM((8, width), f32),
-            pltpu.VMEM((2, 8, width), f32),
+            pltpu.VMEM((1, width), f32),
+            pltpu.VMEM((2, 1, width), f32),
             pltpu.VMEM((3 * heads, rows, width), bf16),
             pltpu.VMEM((2, tiles, TILE, width), bf16),
             pltpu.VMEM((2, tiles, TILE, width), bf16),

time: 27.6 us -> 27.2 us (0.986); the launches traced: 27.2 us -> 27.1 us
  no operation moved by 1% of the time
where the time goes in v11:
time: 27.2 us; the launch traced here: 27.1 us
  Pallas kernels  27.1 us (100%)
    pallas_call x1, Pallas kernels, on_star(): pl.pallas_call(star_kernel, out_shape=[jax.ShapeDtypeStruct(*each) for ea...  25.9 us
    pallas_call x1, Pallas kernels, on_star(): pl.pallas_call(finish_kernel, out_shape=jax.ShapeDtypeStruct((rows, featu...  1.17 us

profile of v11, /device:TPU:0, one launch (start us, length us, event | category | flops | bytes accessed | tf_op | source)
XLA Modules:
  0.0 27.1 jit_solution(9235238548688188380)
XLA Ops:
  0.0 25.9 %shard_map.73 = (bf16[128,2048]{1,0:T(8,128)(2,1)S(1)}, bf16[256,256]{1,0:T(8,128)(2,1)S(1)}, f32[384,2048]{1,0:T(8,128)S(1)}, bf16[256,2048]{1,0:T(8,128)(2,1)S...) custom-call(s32[384]{0:T(512)} %halt_hbm.1, ...), custom_call_target="tpu_custom_call" | custom-call | tf_op jit(solution)/shard_map/pallas_call | solution.py:489
  25.9 1.2 %shard_map.74 = bf16[384,2048]{1,0:T(8,128)(2,1)} custom-call(bf16[128,2048]{1,0:T(8,128)(2,1)S(1)} %get-tuple-element.12.first_ref, bf16[256,256]{1,0:T(8,128)(2,1)S(1)} %get-tuple-element.13.left_ref, f32[384,2048]{1,0:T(8,128)S(1)} %get-tuple-element.14.update, bf16[256,2048]{1,0:T(8,128)(2,1)S(1)} %get-tuple-element.15.w_last, ...), custom_call_target="tpu_custom_call" | custom-call | tf_op jit(solution)/shard_map/pallas_call | solution.py:522
